TPU v7x, 8 devices: a whole 2x2x1 slice. The times are simulated.
8 devices in a mesh: batch: 2 (over z, y), dap: 4 (over x, core).
Axes of the slice: x: 2, y: 2, z: 1, core: 2. Of those that a mesh axis runs over, the one named last changes fastest.
Arguments:
- z_pair: bfloat16 [1024, 512, 128], P(('batch', 'dap')), parts along dimension 0
- pair_mask: int32 [1024, 512], P(('batch', 'dap')), parts along dimension 0
- dz_out: bfloat16 [1024, 512, 128], P(('batch', 'dap')), parts along dimension 0
- ln_in_scale: bfloat16 [128], replicated
- ln_in_offset: bfloat16 [128], replicated
- w_in: bfloat16 [128, 512], replicated
- b_in: bfloat16 [512], replicated
- ln_out_scale: bfloat16 [128], replicated
- ln_out_offset: bfloat16 [128], replicated
- w_out: bfloat16 [128, 128], replicated
- b_out: bfloat16 [128], replicated
- w_gate: bfloat16 [128, 128], replicated
- b_gate: bfloat16 [128], replicated
Outputs:
- output 1: bfloat16 [1024, 512, 128], P(('batch', 'dap')), parts along dimension 0
- output 2: bfloat16 [256], P('batch'), parts along dimension 0
- output 3: bfloat16 [256], P('batch'), parts along dimension 0
- output 4: bfloat16 [256, 512], P('batch'), parts along dimension 0
- output 5: bfloat16 [1024], P('batch'), parts along dimension 0
- output 6: bfloat16 [256], P('batch'), parts along dimension 0
- output 7: bfloat16 [256], P('batch'), parts along dimension 0
- output 8: bfloat16 [256, 128], P('batch'), parts along dimension 0
- output 9: bfloat16 [256], P('batch'), parts along dimension 0
- output 10: bfloat16 [256, 128], P('batch'), parts along dimension 0
- output 11: bfloat16 [256], P('batch'), parts along dimension 0
There are 2 independent parts. A program takes and returns all parts, laid end to end along the dimension named above; an argument that names none is the same for every part.
All inputs are finite; a program needn't handle non-finite values.
Results may differ from a plain program's by a relative error of at most 0.0133434.
Values are sent between devices in bfloat16 or wider.
A program may use at most 1 GiB of HBM per device.

v0:
```python
import functools
import jax
import jax.numpy as jnp
from jax import lax
from jax.experimental import pallas as pl
from jax.experimental.pallas import tpu as pltpu
from jax.sharding import PartitionSpec as P

LN_EPS = 1e-5
F32 = jnp.float32
BF16 = jnp.bfloat16
LANES = 128
ROWS = 16
CH_STEP = 8
VMEM_LIMIT = 60 * 1024 * 1024


def sigmoid(x_val):
    return 1.0 / (1.0 + jnp.exp(-x_val))


def col_mean(x_val):
    return jnp.sum(x_val, axis=0, keepdims=True) * (1.0 / x_val.shape[0])


def dot_nn(lhs, rhs):
    return jnp.dot(lhs, rhs, preferred_element_type=F32)


def dot_nt(lhs, rhs):
    return lax.dot_general(lhs, rhs, (((1,), (1,)), ((), ())), preferred_element_type=F32)


def dot_tn(lhs, rhs):
    return lax.dot_general(lhs, rhs, (((0,), (0,)), ((), ())), preferred_element_type=F32)


def input_norm(z_rows, scale, offset):
    z_t = jnp.transpose(z_rows.astype(F32))
    centered = z_t - col_mean(z_t)
    inv_std = lax.rsqrt(col_mean(centered * centered) + LN_EPS)
    x_hat = centered * inv_std
    return x_hat, inv_std, (x_hat * scale + offset).astype(BF16)


def project_kernel(keep_norm, z_ref, mask_ref, w_ref, bias_ref, scale_ref, offset_ref, *refs):
    refs = refs[-5:] if keep_norm else refs[-4:]
    a_ref, b_ref = refs[:2]
    scr_a, scr_b = refs[-2:]
    n_lane = z_ref.shape[1] // LANES
    chans = z_ref.shape[2]
    pitch = ROWS + 1
    plane = chans * pitch

    def row(i, carry):
        for half in range(n_lane // 2):
            cols = slice(half * 256, half * 256 + 256)
            _, _, znt = input_norm(z_ref[i, cols, :], scale_ref[...], offset_ref[...])
            if keep_norm:
                refs[2][i, cols, :] = jnp.transpose(znt)
            proj = dot_nn(w_ref[...], znt) + bias_ref[...]
            mask_f = jnp.concatenate([mask_ref[i, half * 2 + t] for t in range(2)], axis=1).astype(F32)
            act_a = mask_f * sigmoid(proj[2 * chans:3 * chans]) * proj[:chans]
            act_b = mask_f * sigmoid(proj[3 * chans:]) * proj[chans:2 * chans]
            for t in range(2):
                base = (half * 2 + t) * plane
                part = slice(t * LANES, (t + 1) * LANES)
                scr_a[pl.ds(base + i, chans, stride=pitch), :] = act_a[:, part]
                scr_b[pl.ds(base + i, chans, stride=pitch), :] = act_b[:, part]
        return carry

    lax.fori_loop(0, ROWS, row, 0)

    def pack(c, carry):
        for t in range(n_lane):
            lanes = slice(t * LANES, (t + 1) * LANES)
            at = t * plane + c * pitch
            a_ref[c, :, lanes] = scr_a[pl.ds(at, ROWS), :].astype(BF16)
            b_ref[c, :, lanes] = scr_b[pl.ds(at, ROWS), :].astype(BF16)
        return carry

    lax.fori_loop(0, chans, pack, 0, unroll=4)


def project(z_rows, mask_rows, first, rows, w_t, bias, scale, offset, keep_norm, after=()):
    _, n_col, chans = z_rows.shape
    z_from, m_from = (0 if z_rows.shape[0] == rows else first // ROWS), first // ROWS
    full = lambda arr: pl.BlockSpec(arr.shape, lambda s: (0,) * arr.ndim)
    act = jax.ShapeDtypeStruct((chans, rows, n_col), BF16)
    act_spec = pl.BlockSpec((chans, ROWS, n_col), lambda s: (0, s, 0))
    out_shape = [act, act]
    out_specs = [act_spec, act_spec]
    pair_spec = pl.BlockSpec((ROWS, n_col, chans), lambda s: (s + z_from, 0, 0))
    if keep_norm:
        out_shape.append(jax.ShapeDtypeStruct((rows, n_col, chans), BF16))
        out_specs.append(pair_spec)
    scratch = pltpu.VMEM((n_col // LANES * chans * (ROWS + 1), LANES), F32)
    return pl.pallas_call(
        functools.partial(project_kernel, keep_norm),
        grid=(rows // ROWS,),
        in_specs=[
            pair_spec,
            pl.BlockSpec((ROWS,) + mask_rows.shape[1:], lambda s: (s + m_from, 0, 0, 0)),
            full(w_t), full(bias), full(scale), full(offset)] + [pl.BlockSpec(memory_space=pl.ANY)] * len(after),
        out_specs=out_specs,
        out_shape=out_shape,
        scratch_shapes=[scratch, scratch],
        compiler_params=pltpu.CompilerParams(vmem_limit_bytes=VMEM_LIMIT),
        cost_estimate=pl.CostEstimate(flops=rows * 2 * 10 ** 8, bytes_accessed=rows * 2 ** 19, transcendentals=0),
        name='project',
    )(z_rows, mask_rows, w_t, bias, scale, offset, *after)


def middle_kernel(n_mul, n_mid, idx_ref, a_ref, b0_ref, b1_ref, zn0_ref, zn1_ref, dy0_ref, dy1_ref, wg_ref, bg_ref, wo_ref, wot_ref, bo_ref, scale_ref, offset_ref, *refs):
    do0_ref, do1_ref, gl_ref, dwo_ref, dwg_ref, vec_ref, scr = refs[-7:]
    step = pl.program_id(0)
    tile = LANES
    half = tile // 2
    pitch = tile + 1
    chans = wo_ref.shape[0]

    @pl.when(step == 0)
    def _():
        dwo_ref[...] = jnp.zeros_like(dwo_ref)
        dwg_ref[...] = jnp.zeros_like(dwg_ref)
        vec_ref[...] = jnp.zeros_like(vec_ref)

    @pl.when(step < n_mul)
    def _():
        for j in range(CH_STEP):
            at = (step * CH_STEP + j) * pitch
            scr[pl.ds(at, tile), :] = dot_nt(a_ref[j], jnp.concatenate([b0_ref[j], b1_ref[j]], axis=0))

    @pl.when((step >= n_mul) & (step < n_mul + n_mid))
    def _():
        first = (step - n_mul) * ROWS

        def pair(h, carry):
            r0 = first + 2 * h
            tri = jnp.concatenate([scr[pl.ds(r0 + t, chans, stride=pitch), :] for t in range(2)], axis=1)
            centered = tri - col_mean(tri)
            inv_std = lax.rsqrt(col_mean(centered * centered) + LN_EPS)
            o_hat = centered * inv_std
            o_norm = (o_hat * scale_ref[...] + offset_ref[...]).astype(BF16)
            update = (dot_nn(wot_ref[...], o_norm) + bo_ref[...]).astype(BF16).astype(F32)
            zn = jnp.concatenate([ref[2 * h + t] for t in range(2) for ref in (zn0_ref, zn1_ref)], axis=0)
            sig_g = sigmoid(dot_nt(wg_ref[...], zn) + bg_ref[...])
            dy_t = jnp.transpose(jnp.concatenate([ref[2 * h + t].astype(F32) for t in range(2) for ref in (dy0_ref, dy1_ref)], axis=0))
            d_update = (sig_g * dy_t).astype(BF16)
            d_gate = dy_t * update * sig_g * (1.0 - sig_g)
            gate16 = d_gate.astype(BF16)
            d_onorm = dot_nn(wo_ref[...], d_update).astype(BF16).astype(F32)
            grad_hat = d_onorm * scale_ref[...]
            d_tri = inv_std * (grad_hat - col_mean(grad_hat) - o_hat * col_mean(grad_hat * o_hat))
            d_upf = d_update.astype(F32)
            d_sc = d_onorm * o_hat
            for t in range(2):
                part = slice(t * tile, (t + 1) * tile)
                scr[pl.ds(r0 + t, chans, stride=pitch), :] = d_tri[:, part]
                gl_ref[2 * h + t] = gate16[:, part]
            vec_ref[0] += d_sc[:, :tile] + d_sc[:, tile:]
            vec_ref[1] += d_onorm[:, :tile] + d_onorm[:, tile:]
            vec_ref[2] += d_upf[:, :tile] + d_upf[:, tile:]
            vec_ref[3] += d_gate[:, :tile] + d_gate[:, tile:]
            dwo_ref[...] += dot_nt(o_norm, d_update)
            dwg_ref[...] += dot_nn(gate16, zn)
            return carry

        lax.fori_loop(0, ROWS // 2, pair, 0)

    @pl.when(step >= n_mul + n_mid)
    def _():
        for j in range(CH_STEP):
            at = ((step - n_mul - n_mid) * CH_STEP + j) * pitch
            do_t = jnp.transpose(scr[pl.ds(at, tile), :]).astype(BF16)
            do0_ref[j] = do_t[:half]
            do1_ref[j] = do_t[half:]


def middle(pieces, act_a, b_parts, zn, dy_rows, wg_t, bg, wo, wo_t, bo, scale, offset, after=()):
    chans, rows, n_col = act_a.shape
    half = LANES // 2
    n_mul = chans // CH_STEP
    n_mid = rows // ROWS
    mul_at = lambda s: jnp.minimum(s, n_mul - 1)
    mid_at = lambda s: jnp.clip(s - n_mul, 0, n_mid - 1)
    out_at = lambda s: jnp.maximum(s - n_mul - n_mid, 0)
    full = lambda shape: pl.BlockSpec(shape, lambda s, q: (0,) * len(shape))
    part_spec = lambda at: pl.BlockSpec((CH_STEP, half, n_col), lambda s, q: (mul_at(s), at, 0))
    piece_spec = lambda n: pl.BlockSpec((ROWS, half, chans), lambda s, q: (mid_at(s), q[n], 0))
    do_spec = pl.BlockSpec((CH_STEP, half, rows), lambda s, q: (out_at(s), 0, 0))
    do_type = jax.ShapeDtypeStruct((chans, half, rows), BF16)
    mats = jax.ShapeDtypeStruct((chans, chans), F32)
    return pl.pallas_call(
        functools.partial(middle_kernel, n_mul, n_mid),
        grid_spec=pltpu.PrefetchScalarGridSpec(
            num_scalar_prefetch=1,
            grid=(2 * n_mul + n_mid,),
            in_specs=[
                pl.BlockSpec((CH_STEP, rows, n_col), lambda s, q: (mul_at(s), 0, 0)),
                part_spec(b_parts[0][1]), part_spec(b_parts[1][1]),
                piece_spec(0), piece_spec(1), piece_spec(0), piece_spec(1),
                full(wg_t.shape), full(bg.shape), full(wo.shape), full(wo_t.shape), full(bo.shape), full(scale.shape), full(offset.shape)]
            + [pl.BlockSpec(memory_space=pl.ANY)] * len(after),
            out_specs=[
                do_spec, do_spec,
                pl.BlockSpec((ROWS, chans, LANES), lambda s, q: (mid_at(s), 0, 0)),
                full((chans, chans)), full((chans, chans)), full((4, chans, LANES))],
            scratch_shapes=[pltpu.VMEM((chans * (LANES + 1), LANES), F32)],
        ),
        out_shape=[
            do_type, do_type,
            jax.ShapeDtypeStruct((rows, chans, LANES), BF16),
            mats, mats, jax.ShapeDtypeStruct((4, chans, LANES), F32)],
        compiler_params=pltpu.CompilerParams(vmem_limit_bytes=VMEM_LIMIT),
        cost_estimate=pl.CostEstimate(flops=25 * 10 ** 9, bytes_accessed=48 * 2 ** 20, transcendentals=0),
        name='middle',
    )(pieces, act_a, b_parts[0][0], b_parts[1][0], zn, zn, dy_rows, dy_rows, wg_t, bg, wo, wo_t, bo, scale, offset, *after)


def grad_a_kernel(n_do, n_act, *refs):
    grads, acts, mask_ref, out_ref = refs[:n_do], refs[n_do:n_do + n_act], refs[n_do + n_act], refs[-1]
    for j in range(out_ref.shape[0]):
        lhs = jnp.concatenate([g[j] for g in grads], axis=0)
        rhs = jnp.concatenate([act[j] for act in acts], axis=0)
        out_ref[j] = (dot_tn(lhs, rhs) * mask_ref[...]).astype(BF16)


def grad_a(grads, acts, mask_f):
    chans, _, rows = grads[0].shape
    n_col = acts[0].shape[2]
    block = lambda arr: pl.BlockSpec((CH_STEP,) + arr.shape[1:], lambda s: (s, 0, 0))
    return pl.pallas_call(
        functools.partial(grad_a_kernel, len(grads), len(acts)),
        grid=(chans // CH_STEP,),
        in_specs=[block(arr) for arr in list(grads) + list(acts)] + [pl.BlockSpec(mask_f.shape, lambda s: (0, 0))],
        out_specs=pl.BlockSpec((CH_STEP, rows, n_col), lambda s: (s, 0, 0)),
        out_shape=jax.ShapeDtypeStruct((chans, rows, n_col), BF16),
        compiler_params=pltpu.CompilerParams(vmem_limit_bytes=VMEM_LIMIT),
        cost_estimate=pl.CostEstimate(flops=15 * 10 ** 9, bytes_accessed=96 * 2 ** 20, transcendentals=0),
        name='grad_a',
    )(*grads, *acts, mask_f)


def grad_b_kernel(n_do, n_act, *refs):
    grads, acts, mask_ref, out_ref = refs[:n_do], refs[n_do:n_do + n_act], refs[n_do + n_act], refs[-1]
    for j in range(out_ref.shape[0]):
        lhs = jnp.concatenate([g[j] for g in grads], axis=1)
        rhs = jnp.concatenate([act[j] for act in acts], axis=0)
        out_ref[j] = (dot_nn(lhs, rhs) * mask_ref[...]).astype(BF16)


def grad_b(grads, acts, mask_f, part, after=()):
    chans, rows, _ = grads[0].shape
    n_col = acts[0].shape[2]
    block = lambda arr: pl.BlockSpec((CH_STEP,) + arr.shape[1:], lambda s: (s, 0, 0))
    return pl.pallas_call(
        functools.partial(grad_b_kernel, len(grads), len(acts)),
        grid=(chans // CH_STEP,),
        in_specs=[block(arr) for arr in list(grads) + list(acts)] + [pl.BlockSpec((rows, n_col), lambda s: (part, 0))]
        + [pl.BlockSpec(memory_space=pl.ANY)] * len(after),
        out_specs=pl.BlockSpec((CH_STEP, rows, n_col), lambda s: (s, 0, 0)),
        out_shape=jax.ShapeDtypeStruct((chans, rows, n_col), BF16),
        compiler_params=pltpu.CompilerParams(vmem_limit_bytes=VMEM_LIMIT),
        cost_estimate=pl.CostEstimate(flops=8 * 10 ** 9, bytes_accessed=76 * 2 ** 20, transcendentals=0),
        name='grad_b',
    )(*grads, *acts, mask_f, *after)


def final_kernel(seeded, q_ref, z_ref, dy_ref, da_ref, db_ref, gl0, gl1, gl2, gl3, w_ref, wb_ref, bias_ref, scale_ref, offset_ref, *refs):
    dz_ref, dw_ref, dbin_ref, vec_ref, scr_a, scr_b = refs[-6:]
    gls = (gl0, gl1, gl2, gl3)
    chans = z_ref.shape[2]
    n_lane = z_ref.shape[1] // LANES
    side = LANES // 2
    pitch = ROWS + 1
    plane = chans * pitch

    @pl.when(pl.program_id(0) == 0)
    def _():
        if seeded:
            for ref, seed in zip((dw_ref, dbin_ref, vec_ref), refs[:3]):
                ref[...] = seed[...]
        else:
            dw_ref[...] = jnp.zeros_like(dw_ref)
            dbin_ref[...] = jnp.zeros_like(dbin_ref)
            vec_ref[...] = jnp.zeros_like(vec_ref)

    def unpack(c, carry):
        for t in range(n_lane):
            lanes = slice(t * LANES, (t + 1) * LANES)
            at = t * plane + c * pitch
            scr_a[pl.ds(at, ROWS), :] = da_ref[c, :, lanes].astype(F32)
            scr_b[pl.ds(at, ROWS), :] = db_ref[c, :, lanes].astype(F32)
        return carry

    lax.fori_loop(0, chans, unpack, 0, unroll=4)

    def row(i, carry):
        for half in range(n_lane // 2):
            qs = [q_ref[2 * half + t] for t in range(2)]
            offs = [pl.multiple_of(q * LANES, LANES) for q in qs]
            z_rows = jnp.concatenate([z_ref[i, pl.ds(off, LANES), :] for off in offs], axis=0)
            x_hat, inv_std, znt = input_norm(z_rows, scale_ref[...], offset_ref[...])
            proj = dot_nn(w_ref[...], znt) + bias_ref[...]
            grad_a = jnp.concatenate([scr_a[pl.ds(q * plane + i, chans, stride=pitch), :] for q in qs], axis=1)
            grad_b = jnp.concatenate([scr_b[pl.ds(q * plane + i, chans, stride=pitch), :] for q in qs], axis=1)
            sig_a = sigmoid(proj[2 * chans:3 * chans])
            sig_b = sigmoid(proj[3 * chans:])
            gs_a = grad_a * sig_a
            gs_b = grad_b * sig_b
            d_proj = jnp.concatenate([gs_a, gs_b, gs_a * proj[:chans] * (1.0 - sig_a), gs_b * proj[chans:2 * chans] * (1.0 - sig_b)], axis=0)
            dbin_ref[...] += d_proj[:, :LANES] + d_proj[:, LANES:]
            gate = [gls[2 * half + t][i] for t in range(2)]
            if half:
                gate = [g[:, part] for part in (slice(0, side), slice(side, LANES)) for g in gate]
            gate = jnp.concatenate(gate, axis=1)
            grad16 = d_proj.astype(BF16)
            dw_ref[...] += dot_nt(grad16, znt)
            d_znorm = dot_nn(wb_ref[...], jnp.concatenate([grad16, gate], axis=0)).astype(BF16).astype(F32)
            d_sc = d_znorm * x_hat
            vec_ref[0] += d_sc[:, :LANES] + d_sc[:, LANES:]
            vec_ref[1] += d_znorm[:, :LANES] + d_znorm[:, LANES:]
            grad_hat = d_znorm * scale_ref[...]
            d_in = inv_std * (grad_hat - col_mean(grad_hat) - x_hat * col_mean(grad_hat * x_hat))
            d_rows = jnp.transpose(d_in)
            for t in range(2):
                out = d_rows[t * LANES:(t + 1) * LANES] + dy_ref[i, pl.ds(offs[t], LANES), :].astype(F32)
                dz_ref[i, pl.ds(offs[t], LANES), :] = out.astype(BF16)
        return carry

    lax.fori_loop(0, ROWS, row, 0)


def final(q_all, z_rows, dy_rows, d_a, d_b, gates, w_t, w_back, bias, scale, offset, first, d_z=None, seeds=()):
    _, n_col, chans = z_rows.shape
    n_step = d_b.shape[1] // ROWS
    at = first // ROWS
    full = lambda shape: pl.BlockSpec(shape, lambda s, q: (0,) * len(shape))
    pair_spec = pl.BlockSpec((ROWS, n_col, chans), lambda s, q: (s + at, 0, 0))
    scratch = pltpu.VMEM((n_col // LANES * chans * (ROWS + 1), LANES), F32)
    sums = [(4 * chans, chans), (4 * chans, LANES), (2, chans, LANES)]
    args = [q_all, z_rows, dy_rows, d_a, d_b, *gates, w_t, w_back, bias, scale, offset, *seeds]
    in_specs = ([pair_spec, pair_spec, pl.BlockSpec((chans, ROWS, n_col), lambda s, q: (0, s + at, 0)),
                 pl.BlockSpec((chans, ROWS, n_col), lambda s, q: (0, s, 0))]
                + [pl.BlockSpec((ROWS, chans, LANES), lambda s, q: (s + at, 0, 0))] * 4
                + [full(w_t.shape), full(w_back.shape), full(bias.shape), full(scale.shape), full(offset.shape)]
                + [full(seed.shape) for seed in seeds])
    alias = {}
    if d_z is not None:
        alias = {len(args): 0}
        args.append(d_z)
        in_specs.append(pl.BlockSpec(memory_space=pl.ANY))
    return pl.pallas_call(
        functools.partial(final_kernel, bool(seeds)),
        grid_spec=pltpu.PrefetchScalarGridSpec(
            num_scalar_prefetch=1,
            grid=(n_step,),
            in_specs=in_specs,
            out_specs=[pair_spec] + [full(shape) for shape in sums],
            scratch_shapes=[scratch, scratch],
        ),
        out_shape=[jax.ShapeDtypeStruct(z_rows.shape, BF16)] + [jax.ShapeDtypeStruct(shape, F32) for shape in sums],
        input_output_aliases=alias,
        compiler_params=pltpu.CompilerParams(vmem_limit_bytes=VMEM_LIMIT),
        cost_estimate=pl.CostEstimate(flops=30 * 10 ** 9, bytes_accessed=64 * 2 ** 20, transcendentals=0),
        name='final',
    )(*args)


def lane_bcast(vec, width):
    return jnp.broadcast_to(vec.astype(F32)[:, None], (vec.shape[0], width))


def local_step(z_loc, mask_loc, dy_loc, ln_in_scale, ln_in_offset, w_in, b_in, ln_out_scale, ln_out_offset, w_out, b_out, w_gate, b_gate):
    n_dap = lax.axis_size('dap')
    me = lax.axis_index('dap')
    swap = lambda arr, bit: lax.ppermute(arr, 'dap', [(d, d ^ bit) for d in range(n_dap)])
    w_t = w_in.T
    bias = lane_bcast(b_in, 256)
    in_sc, in_of = lane_bcast(ln_in_scale, 256), lane_bcast(ln_in_offset, 256)
    out_sc, out_of = lane_bcast(ln_out_scale, 256), lane_bcast(ln_out_offset, 256)
    z_far = swap(z_loc, 2)
    rows = z_loc.shape[0]
    part = rows // 2
    mask_f = mask_loc.astype(F32)
    mask_loc = mask_loc.reshape(rows, -1, 1, LANES)
    mask_far = swap(mask_loc, 2)
    z_far = [swap(z_loc[:part], 2)]
    z_far.append(swap(lax.optimization_barrier(z_loc)[part:], 2))
    weights = (w_t, bias, in_sc, in_of)
    a_0, b_0, zn = project(z_loc, mask_loc, 0, rows, *weights, True)
    b_1 = swap(b_0, 1)
    a_1 = swap(a_0, 1)
    blocks = [me ^ r for r in range(n_dap)]
    tail = (zn, dy_loc, w_gate.T, lane_bcast(b_gate, 256), w_out, w_out.T, lane_bcast(b_out, 256), out_sc, out_of)
    pieces = lambda *vals: jnp.stack(vals).astype(jnp.int32)
    mids = [middle(pieces(2 * blocks[0], 2 * blocks[0] + 1), a_0, [(b_0, 0), (b_0, 1)], *tail)]
    mids.append(middle(pieces(2 * blocks[1], 2 * blocks[1] + 1), a_0, [(b_1, 0), (b_1, 1)], *tail, after=(mids[0][5],)))
    near_out = [swap(mids[1][0], 1), swap(mids[1][1], 1)]
    a_2, b_2, a_3, b_3, far_out = [], [], [], [], []
    for h in range(2):
        a_h, b_h = project(z_far[h], mask_far, h * part, part, *weights, False, after=(mids[-1][5],))
        b_3.append(swap(b_h, 1))
        a_3.append(swap(a_h, 1))
        a_2.append(a_h)
        b_2.append(b_h)
        mids.append(middle(pieces(2 * blocks[2] + h, 2 * blocks[3] + h), a_0, [(b_2[h], 0), (b_3[h], 0)], *tail, after=(a_h,)))
        far_out.append([swap(mids[2 + h][0], 2), swap(mids[2 + h][1], 3)])
    grads = [m[n] for m in mids for n in range(2)]
    d_a = grad_a(grads, [b_0, b_1, b_2[0], b_3[0], b_2[1], b_3[1]], mask_f)
    w_back = jnp.concatenate([w_in, w_gate], axis=1)
    acts = [a_0, a_1, *a_2, *a_3]
    d_z, seeds = None, ()
    for h in range(2):
        d_b = grad_b([mids[0][h], near_out[h], far_out[h][0], far_out[h][1]], acts, mask_f, h, after=(d_a,) if h == 0 else (seeds[2],))
        d_z, *seeds = final(jnp.stack(blocks).astype(jnp.int32), z_loc, dy_loc, d_a, d_b, [m[2] for m in mids], w_t, w_back, bias, in_sc, in_of,
                            h * part, d_z, seeds)
    dw_t, dbin, vecs = seeds
    d_wo = sum(m[3] for m in mids)
    d_wg = sum(m[4] for m in mids).T
    vec_mid = jnp.sum(sum(m[5] for m in mids), axis=-1)
    vec_in = jnp.sum(vecs, axis=-1)
    summed = lax.psum((vec_in[0], vec_in[1], dw_t, jnp.sum(dbin, axis=-1), vec_mid[0], vec_mid[1], d_wo, vec_mid[2], d_wg, vec_mid[3]), 'dap')
    summed = list(summed)
    summed[2] = summed[2].T
    return (d_z,) + tuple(piece.astype(BF16) for piece in summed)


def solution(mesh):
    pair_spec = P(('batch', 'dap'), None, None)
    mask_spec = P(('batch', 'dap'), None)
    vec_rep = P(None)
    mat_rep = P(None, None)
    vec_part = P('batch')
    mat_part = P('batch', None)
    in_specs = (pair_spec, mask_spec, pair_spec, vec_rep, vec_rep, mat_rep, vec_rep, vec_rep, vec_rep, mat_rep, vec_rep, mat_rep, vec_rep)
    out_specs = (pair_spec, vec_part, vec_part, mat_part, vec_part, vec_part, vec_part, mat_part, vec_part, mat_part, vec_part)
    return jax.shard_map(local_step, mesh=mesh, in_specs=in_specs, out_specs=out_specs, check_vma=False)
```

profile of v0, /device:TPU:0, one launch (start us, length us, event | category | flops | bytes accessed | tf_op | source)
XLA Modules:
  0.0 926.7 jit_solution(6206534324704958599)
XLA Ops:
  0.6 2.0 reshape.32.mask_ref
  2.6 1.7 copy.25
  4.3 1.6 broadcast_in_dim.14.bias_ref
  5.9 1.4 broadcast_in_dim.15.scale_ref
  7.3 1.4 broadcast_in_dim.16.offset_ref
  8.7 80.8 %project.3 = (bf16[128,128,512]{2,1,0:T(8,128)(2,1)}, bf16[128,128,512]{2,1,0:T(8,128)(2,1)}, bf16[128,512,128]{2,1,0:T(8,128)(2,1)}) custom-call(bf16[128,512,128]{2,1,0:T(8,128)(2,1)} %z_ref.5, s32[128,4,1,128]{3,2,1,0:T(1,128)} %reshape.32.mask_ref, bf16[512,128]{1,0:T(8,128)(2,1)} %bitcast.40, f32[512,256]{1,0:T(8,128)} %broadcast_in_dim.14.bias_ref, ...), custom_call_target="tpu_custom_call" | custom-call | flops 25600000000 | bytes 67108864 | tf_op jit(solution)/shard_map/project/pallas_call | solution.py:98
  90.4 7.6 slice.24
  98.0 2.6 collective-permute-start.1
  106.2 55.3 %middle.4 = (bf16[128,64,128]{2,1,0:T(8,128)(2,1)}, bf16[128,64,128]{2,1,0:T(8,128)(2,1)}, bf16[128,128,128]{2,1,0:T(8,128)(2,1)}, f32[128,128]{1,0:T(8,128)}, f...) custom-call(s32[2]{0:T(128)} %pad_add_fusion.1.idx_ref, bf16[128,128,512]{2,1,0:T(8,128)(2,1)} %get-tuple-element.50.a_ref.refs_4_, ...), custom_call_target="tpu_custom_call" | custom-call | flops 24999999488 | bytes 50331648 | tf_op jit(solution)/shard_map/middle/pallas_call | solution.py:194
  161.5 55.3 %middle.5 = (bf16[128,64,128]{2,1,0:T(8,128)(2,1)}, bf16[128,64,128]{2,1,0:T(8,128)(2,1)}, bf16[128,128,128]{2,1,0:T(8,128)(2,1)}, f32[128,128]{1,0:T(8,128)}, f...) custom-call(s32[2]{0:T(128)} %pad_add_fusion.2.idx_ref, bf16[128,128,512]{2,1,0:T(8,128)(2,1)} %get-tuple-element.50.a_ref.refs_4_, ...), custom_call_target="tpu_custom_call" | custom-call | flops 24999999488 | bytes 50331648 | tf_op jit(solution)/shard_map/middle/pallas_call | solution.py:194
  216.9 70.6 %collective-permute-done.2.mask_ref = s32[128,4,1,128]{3,2,1,0:T(1,128)S(1)} collective-permute-done((s32[128,4,1,128]{3,2,1,0:T(1,128)S(1)}, s32[128,4,1,128]{3,2,1,0:T(1,128)S(1)}, u32[]{:S(2)}, u32[]{:S(2)}) %collective-permute-start.2) | collective-permute-done | bytes 262176 | tf_op jit(solution)/shard_map/ppermute | solution.py:378
  288.2 41.6 %project.4 = (bf16[128,64,512]{2,1,0:T(8,128)(2,1)}, bf16[128,64,512]{2,1,0:T(8,128)(2,1)}) custom-call(bf16[64,512,128]{2,1,0:T(8,128)(2,1)} %collective-permute-done.1.z_ref, s32[128,4,1,128]{3,2,1,0:T(1,128)} %copy-done.20, bf16[512,128]{1,0:T(8,128)(2,1)} %bitcast.41, f32[512,256]{1,0:T(8,128)} %broadcast_in_dim.14.bias_ref, ...), custom_call_target="tpu_custom_call" | custom-call | flops 12800000000 | bytes 33554432 | tf_op jit(solution)/shard_map/project/pallas_call | solution.py:98
  329.8 7.7 slice.32
  337.5 1.7 collective-permute-start.4
  340.1 3.2 collective-permute-done.3.b1_ref.refs_11_
  343.3 55.4 %middle.6 = (bf16[128,64,128]{2,1,0:T(8,128)(2,1)}, bf16[128,64,128]{2,1,0:T(8,128)(2,1)}, bf16[128,128,128]{2,1,0:T(8,128)(2,1)}, f32[128,128]{1,0:T(8,128)}, f...) custom-call(s32[2]{0:T(128)} %pad_add_fusion.3.idx_ref, bf16[128,128,512]{2,1,0:T(8,128)(2,1)} %get-tuple-element.50.a_ref.refs_4_, ...), custom_call_target="tpu_custom_call" | custom-call | flops 24999999488 | bytes 50331648 | tf_op jit(solution)/shard_map/middle/pallas_call | solution.py:194
  398.7 122.0 %collective-permute-done.4.z_ref = bf16[64,512,128]{2,1,0:T(8,128)(2,1)} collective-permute-done((bf16[64,512,128]{2,1,0:T(8,128)(2,1)}, bf16[64,512,128]{2,1,0:T(8,128)(2,1)}, u32[]{:S(2)}, u32[]{:S(2)}) %collective-permute-start.4) | collective-permute-done | bytes 8388640 | tf_op jit(solution)/shard_map/ppermute | solution.py:378
  520.7 41.8 %project.5 = (bf16[128,64,512]{2,1,0:T(8,128)(2,1)}, bf16[128,64,512]{2,1,0:T(8,128)(2,1)}) custom-call(bf16[64,512,128]{2,1,0:T(8,128)(2,1)} %collective-permute-done.4.z_ref, s32[128,4,1,128]{3,2,1,0:T(1,128)} %copy-done.20, bf16[512,128]{1,0:T(8,128)(2,1)} %bitcast.42, f32[512,256]{1,0:T(8,128)} %broadcast_in_dim.14.bias_ref, ...), custom_call_target="tpu_custom_call" | custom-call | flops 12800000000 | bytes 33554432 | tf_op jit(solution)/shard_map/project/pallas_call | solution.py:98
  565.5 1.7 collective-permute-start.13
  567.3 8.8 collective-permute-done.5.b1_ref.refs_13_
  576.1 1.5 collective-permute-start.14
  577.6 55.5 %middle.7 = (bf16[128,64,128]{2,1,0:T(8,128)(2,1)}, bf16[128,64,128]{2,1,0:T(8,128)(2,1)}, bf16[128,128,128]{2,1,0:T(8,128)(2,1)}, f32[128,128]{1,0:T(8,128)}, f...) custom-call(s32[2]{0:T(128)} %pad_add_fusion.4.idx_ref, bf16[128,128,512]{2,1,0:T(8,128)(2,1)} %get-tuple-element.50.a_ref.refs_4_, ...), custom_call_target="tpu_custom_call" | custom-call | flops 24999999488 | bytes 50331648 | tf_op jit(solution)/shard_map/middle/pallas_call | solution.py:194
  633.1 1.1 add_reduce_fusion
  635.2 34.9 %grad_a.1.refs_11_.da_ref = bf16[128,128,512]{2,1,0:T(8,128)(2,1)} custom-call(bf16[128,64,128]{2,1,0:T(8,128)(2,1)} %get-tuple-element.53.refs_0_, bf16[128,64,128]{2,1,0:T(8,128)(2,1)} %get-tuple-element.54.refs_1_.refs_0_, bf16[128,64,128]{2,1,0:T(8,128)(2,1)} %get-tuple-element.56.refs_2_, bf16[128,64,128]{2,1,0:T(8,128)(2,1)} %get-tuple-element.57.refs_3_, ...), custom_call_target="tpu_custom_call" | custom-call | flops 15000000512 | bytes 100663296 | tf_op jit(solution)/shard_map/grad_a/pallas_call | solution.py:233
  671.0 1.1 collective-permute-start.8
  672.1 31.5 %grad_b.2.db_ref = bf16[128,64,512]{2,1,0:T(8,128)(2,1)} custom-call(bf16[128,64,128]{2,1,0:T(8,128)(2,1)} %get-tuple-element.53.refs_0_, bf16[128,64,128]{2,1,0:T(8,128)(2,1)} %collective-permute-done.12.refs_1_, bf16[128,64,128]{2,1,0:T(8,128)(2,1)} %collective-permute-done.13.refs_2_, bf16[128,64,128]{2,1,0:T(8,128)(2,1)} %collective-permute-done.14.refs_3_, ...), custom_call_target="tpu_custom_call" | custom-call | flops 8000000000 | bytes 79691776 | tf_op jit(solution)/shard_map/grad_b/pallas_call | solution.py:257
  703.6 85.6 %final.2 = (bf16[128,512,128]{2,1,0:T(8,128)(2,1)}, f32[512,128]{1,0:T(8,128)}, f32[512,128]{1,0:T(8,128)}, f32[2,128,128]{2,1,0:T(8,128)}) custom-call(s32[4]{0:T(128)} %pad_add_fusion.q_ref, bf16[128,512,128]{2,1,0:T(8,128)(2,1)} %z_ref.5, bf16[128,512,128]{2,1,0:T(8,128)(2,1)} %dy_ref.3, bf16[128,128,512]{2,1,0:T(8,128)(2,1)} %grad_a.1.refs_11_.da_ref, ...), custom_call_target="tpu_custom_call" | custom-call | flops 30000001024 | bytes 67108864 | tf_op jit(solution)/shard_map/final/pallas_call | solution.py:354
  789.2 31.5 %grad_b.3.db_ref = bf16[128,64,512]{2,1,0:T(8,128)(2,1)} custom-call(bf16[128,64,128]{2,1,0:T(8,128)(2,1)} %get-tuple-element.54.refs_1_.refs_0_, bf16[128,64,128]{2,1,0:T(8,128)(2,1)} %collective-permute-done.6.refs_1_, bf16[128,64,128]{2,1,0:T(8,128)(2,1)} %collective-permute-done.7.refs_2_, bf16[128,64,128]{2,1,0:T(8,128)(2,1)} %collective-permute-done.8.refs_3_, ...), custom_call_target="tpu_custom_call" | custom-call | flops 8000000000 | bytes 79691776 | tf_op jit(solution)/shard_map/grad_b/pallas_call | solution.py:257
  820.7 85.8 %final.3 = (bf16[128,512,128]{2,1,0:T(8,128)(2,1)}, f32[512,128]{1,0:T(8,128)}, f32[512,128]{1,0:T(8,128)}, f32[2,128,128]{2,1,0:T(8,128)}) custom-call(s32[4]{0:T(128)} %pad_add_fusion.q_ref, bf16[128,512,128]{2,1,0:T(8,128)(2,1)} %z_ref.5, bf16[128,512,128]{2,1,0:T(8,128)(2,1)} %dy_ref.3, ...), custom_call_target="tpu_custom_call", output_to_operand_aliasing={{0}: (17, {})} | custom-call | flops 30000001024 | bytes 67108864 | tf_op jit(solution)/shard_map/final/pallas_call | solution.py:354
  906.5 1.0 reduce_sum.27
  907.6 1.1 reduce_sum.28
  908.7 16.5 %all-reduce.2 = (bf16[128]{0:T(256)(128)(2,1)}, bf16[128]{0:T(256)(128)(2,1)}, bf16[512,128]{1,0:T(8,128)(2,1)S(1)}, bf16[512]{0:T(512)(128)(2,1)}, bf16[128]{0:...) all-reduce(f32[128]{0:T(128)S(1)} %get-tuple-element.115, ...), channel_id=1, replica_groups=mesh['batch'=2,'dap'=4] {'dap'}, use_global_device_ids=true, to_apply=%region_1.0 | all-reduce | flops 99584 | bytes 597504 | tf_op jit(solution)/shard_map/psum | solution.py:424
  (82 shorter events, 14.2 us)
Async XLA Ops:
  89.5 13.7 %copy-start.16 = (bf16[128]{0:T(256)(128)(2,1)S(1)}, bf16[128]{0:T(256)(128)(2,1)}, u32[]{:S(2)}) copy-start(bf16[128]{0:T(256)(128)(2,1)} %param.25) | copy-start | bytes 772
  89.5 14.4 %copy-start.17 = (bf16[128]{0:T(256)(128)(2,1)S(1)}, bf16[128]{0:T(256)(128)(2,1)}, u32[]{:S(2)}) copy-start(bf16[128]{0:T(256)(128)(2,1)} %param.23) | copy-start | bytes 772
  89.5 15.2 %copy-start.18 = (bf16[128]{0:T(256)(128)(2,1)S(1)}, bf16[128]{0:T(256)(128)(2,1)}, u32[]{:S(2)}) copy-start(bf16[128]{0:T(256)(128)(2,1)} %param.20) | copy-start | bytes 772
  89.6 15.9 %copy-start.19 = (bf16[128]{0:T(256)(128)(2,1)S(1)}, bf16[128]{0:T(256)(128)(2,1)}, u32[]{:S(2)}) copy-start(bf16[128]{0:T(256)(128)(2,1)} %param.21) | copy-start | bytes 772
  89.6 71.9 %collective-permute-start = (bf16[128,128,512]{2,1,0:T(8,128)(2,1)}, bf16[128,128,512]{2,1,0:T(8,128)(2,1)}, u32[]{:S(2)}, u32[]{:S(2)}) collective-permute-start(bf16[128,128,512]{2,1,0:T(8,128)(2,1)} %get-tuple-element.51.b0_ref.b1_ref.refs_8_), channel_id=1, source_target_pairs={{0,1},{1,0},{2,3},{3,2},{4,5},{5,4},{6,7},{7,6}} | collective-permute-start | bytes 50331656 | tf_op jit(solution)/shard_map/ppermute | solution.py:378
  98.0 189.4 %collective-permute-start.1 = (bf16[64,512,128]{2,1,0:T(8,128)(2,1)}, bf16[64,512,128]{2,1,0:T(8,128)(2,1)}, u32[]{:S(2)}, u32[]{:S(2)}) collective-permute-start(bf16[64,512,128]{2,1,0:T(8,128)(2,1)} %slice.24), channel_id=1, source_target_pairs={{0,2},{1,3},{2,0},{3,1},{4,6},{5,7},{6,4},{7,5}} | collective-permute-start | bytes 25165832 | tf_op jit(solution)/shard_map/ppermute | solution.py:378
  100.6 186.9 %collective-permute-start.2 = (s32[128,4,1,128]{3,2,1,0:T(1,128)S(1)}, s32[128,4,1,128]{3,2,1,0:T(1,128)S(1)}, u32[]{:S(2)}, u32[]{:S(2)}) collective-permute-start(s32[128,4,1,128]{3,2,1,0:T(1,128)S(1)} %copy-done.5), channel_id=1, source_target_pairs={{0,2},{1,3},{2,0},{3,1},{4,6},{5,7},{6,4},{7,5}} | collective-permute-start | bytes 786440 | tf_op jit(solution)/shard_map/ppermute | solution.py:378
  329.8 13.5 %collective-permute-start.3 = (bf16[128,64,512]{2,1,0:T(8,128)(2,1)}, bf16[128,64,512]{2,1,0:T(8,128)(2,1)}, u32[]{:S(2)}, u32[]{:S(2)}) collective-permute-start(bf16[128,64,512]{2,1,0:T(8,128)(2,1)} %get-tuple-element.59.b0_ref.refs_10_), channel_id=1, source_target_pairs={{0,1},{1,0},{2,3},{3,2},{4,5},{5,4},{6,7},{7,6}} | collective-permute-start | bytes 25165832 | tf_op jit(solution)/shard_map/ppermute | solution.py:378
  337.5 183.2 %collective-permute-start.4 = (bf16[64,512,128]{2,1,0:T(8,128)(2,1)}, bf16[64,512,128]{2,1,0:T(8,128)(2,1)}, u32[]{:S(2)}, u32[]{:S(2)}) collective-permute-start(bf16[64,512,128]{2,1,0:T(8,128)(2,1)} %slice.32), channel_id=1, source_target_pairs={{0,2},{1,3},{2,0},{3,1},{4,6},{5,7},{6,4},{7,5}} | collective-permute-start | bytes 25165832 | tf_op jit(solution)/shard_map/ppermute | solution.py:378
  339.3 226.3 %collective-permute-start.9 = (bf16[128,128,512]{2,1,0:T(8,128)(2,1)}, bf16[128,128,512]{2,1,0:T(8,128)(2,1)}, u32[]{:S(2)}, u32[]{:S(2)}) collective-permute-start(bf16[128,128,512]{2,1,0:T(8,128)(2,1)} %get-tuple-element.50.a_ref.refs_4_), channel_id=1, source_target_pairs={{0,1},{1,0},{2,3},{3,2},{4,5},{5,4},{6,7},{7,6}} | collective-permute-start | bytes 50331656 | tf_op jit(solution)/shard_map/ppermute | solution.py:378
  520.7 42.4 %copy-start.2 = (s32[128,512]{1,0:T(8,128)S(1)}, s32[128,512]{1,0:T(8,128)}, u32[]{:S(2)}) copy-start(s32[128,512]{1,0:T(8,128)} %param.14) | copy-start | bytes 786436
  520.7 44.3 %copy-start.4 = (bf16[128,512]{1,0:T(8,128)(2,1)S(1)}, bf16[128,512]{1,0:T(8,128)(2,1)}, u32[]{:S(2)}) copy-start(bf16[128,512]{1,0:T(8,128)(2,1)} %param.18) | copy-start | bytes 393220
  562.5 13.5 %collective-permute-start.5 = (bf16[128,64,512]{2,1,0:T(8,128)(2,1)}, bf16[128,64,512]{2,1,0:T(8,128)(2,1)}, u32[]{:S(2)}, u32[]{:S(2)}) collective-permute-start(bf16[128,64,512]{2,1,0:T(8,128)(2,1)} %get-tuple-element.64.b0_ref.refs_12_), channel_id=1, source_target_pairs={{0,1},{1,0},{2,3},{3,2},{4,5},{5,4},{6,7},{7,6}} | collective-permute-start | bytes 25165832 | tf_op jit(solution)/shard_map/ppermute | solution.py:378
  562.5 108.0 %collective-permute-start.10 = (bf16[128,64,512]{2,1,0:T(8,128)(2,1)}, bf16[128,64,512]{2,1,0:T(8,128)(2,1)}, u32[]{:S(2)}, u32[]{:S(2)}) collective-permute-start(bf16[128,64,512]{2,1,0:T(8,128)(2,1)} %get-tuple-element.60.refs_0_.refs_6_), channel_id=1, source_target_pairs={{0,1},{1,0},{2,3},{3,2},{4,5},{5,4},{6,7},{7,6}} | collective-permute-start | bytes 25165832 | tf_op jit(solution)/shard_map/ppermute | solution.py:378
  563.1 109.0 %collective-permute-start.11 = (bf16[128,64,512]{2,1,0:T(8,128)(2,1)}, bf16[128,64,512]{2,1,0:T(8,128)(2,1)}, u32[]{:S(2)}, u32[]{:S(2)}) collective-permute-start(bf16[128,64,512]{2,1,0:T(8,128)(2,1)} %get-tuple-element.65.refs_0_.refs_7_), channel_id=1, source_target_pairs={{0,1},{1,0},{2,3},{3,2},{4,5},{5,4},{6,7},{7,6}} | collective-permute-start | bytes 25165832 | tf_op jit(solution)/shard_map/ppermute | solution.py:378
  565.0 68.1 %copy-start.9 = (bf16[128,640]{1,0:T(8,128)(2,1)}, bf16[128,640]{1,0:T(8,128)(2,1)S(1)}, u32[]{:S(2)}) copy-start(bf16[128,640]{1,0:T(8,128)(2,1)S(1)} %constant_dynamic-update-slice_fusion.wb_ref) | copy-start | bytes 491524
  565.0 105.1 %collective-permute-start.12 = (bf16[128,64,128]{2,1,0:T(8,128)(2,1)}, bf16[128,64,128]{2,1,0:T(8,128)(2,1)}, u32[]{:S(2)}, u32[]{:S(2)}) collective-permute-start(bf16[128,64,128]{2,1,0:T(8,128)(2,1)} %get-tuple-element.56.refs_2_), channel_id=1, source_target_pairs={{0,1},{1,0},{2,3},{3,2},{4,5},{5,4},{6,7},{7,6}} | collective-permute-start | bytes 6291464 | tf_op jit(solution)/shard_map/ppermute | solution.py:378
  565.5 105.5 %collective-permute-start.13 = (bf16[128,64,128]{2,1,0:T(8,128)(2,1)}, bf16[128,64,128]{2,1,0:T(8,128)(2,1)}, u32[]{:S(2)}, u32[]{:S(2)}) collective-permute-start(bf16[128,64,128]{2,1,0:T(8,128)(2,1)} %get-tuple-element.61.refs_4_), channel_id=1, source_target_pairs={{0,2},{1,3},{2,0},{3,1},{4,6},{5,7},{6,4},{7,5}} | collective-permute-start | bytes 6291464 | tf_op jit(solution)/shard_map/ppermute | solution.py:378
  576.0 57.0 %copy-start.1 = (f32[4,128,128]{2,1,0:T(8,128)S(1)}, f32[4,128,128]{2,1,0:T(8,128)}, u32[]{:S(2)}) copy-start(f32[4,128,128]{2,1,0:T(8,128)} %get-tuple-element.55.refs_0_) | copy-start | bytes 786436
  576.0 57.1 %copy-start.6 = (f32[4,128,128]{2,1,0:T(8,128)S(1)}, f32[4,128,128]{2,1,0:T(8,128)}, u32[]{:S(2)}) copy-start(f32[4,128,128]{2,1,0:T(8,128)} %get-tuple-element.58.refs_0_) | copy-start | bytes 786436
  576.0 57.1 %copy-start.7 = (f32[4,128,128]{2,1,0:T(8,128)S(1)}, f32[4,128,128]{2,1,0:T(8,128)}, u32[]{:S(2)}) copy-start(f32[4,128,128]{2,1,0:T(8,128)} %get-tuple-element.63.refs_0_) | copy-start | bytes 786436
  576.0 58.2 %copy-start.10 = (f32[128,128]{1,0:T(8,128)S(1)}, f32[128,128]{1,0:T(8,128)}, u32[]{:S(2)}) copy-start(f32[128,128]{1,0:T(8,128)} %get-tuple-element.81) | copy-start | bytes 196612
  576.1 58.2 %copy-start.11 = (f32[128,128]{1,0:T(8,128)S(1)}, f32[128,128]{1,0:T(8,128)}, u32[]{:S(2)}) copy-start(f32[128,128]{1,0:T(8,128)} %get-tuple-element.85) | copy-start | bytes 196612
  576.1 58.2 %copy-start.12 = (f32[128,128]{1,0:T(8,128)S(1)}, f32[128,128]{1,0:T(8,128)}, u32[]{:S(2)}) copy-start(f32[128,128]{1,0:T(8,128)} %get-tuple-element.82) | copy-start | bytes 196612
  576.1 58.2 %copy-start.13 = (f32[128,128]{1,0:T(8,128)S(1)}, f32[128,128]{1,0:T(8,128)}, u32[]{:S(2)}) copy-start(f32[128,128]{1,0:T(8,128)} %get-tuple-element.86) | copy-start | bytes 196612
  576.1 58.2 %copy-start.14 = (f32[128,128]{1,0:T(8,128)S(1)}, f32[128,128]{1,0:T(8,128)}, u32[]{:S(2)}) copy-start(f32[128,128]{1,0:T(8,128)} %get-tuple-element.83) | copy-start | bytes 196612
  576.1 58.2 %copy-start.15 = (f32[128,128]{1,0:T(8,128)S(1)}, f32[128,128]{1,0:T(8,128)}, u32[]{:S(2)}) copy-start(f32[128,128]{1,0:T(8,128)} %get-tuple-element.87) | copy-start | bytes 196612
  576.1 96.0 %collective-permute-start.14 = (bf16[128,64,128]{2,1,0:T(8,128)(2,1)}, bf16[128,64,128]{2,1,0:T(8,128)(2,1)}, u32[]{:S(2)}, u32[]{:S(2)}) collective-permute-start(bf16[128,64,128]{2,1,0:T(8,128)(2,1)} %get-tuple-element.62.refs_5_), channel_id=1, source_target_pairs={{0,3},{1,2},{2,1},{3,0},{4,7},{5,6},{6,5},{7,4}} | collective-permute-start | bytes 6291464 | tf_op jit(solution)/shard_map/ppermute | solution.py:378
  635.2 35.0 %copy-start = (bf16[128,64,128]{2,1,0:T(8,128)(2,1)S(1)}, bf16[128,64,128]{2,1,0:T(8,128)(2,1)}, u32[]{:S(2)}) copy-start(bf16[128,64,128]{2,1,0:T(8,128)(2,1)} %get-tuple-element.57.refs_3_) | copy-start | bytes 6291460
  670.2 119.0 %collective-permute-start.6 = (bf16[128,64,128]{2,1,0:T(8,128)(2,1)S(1)}, bf16[128,64,128]{2,1,0:T(8,128)(2,1)}, u32[]{:S(2)}, u32[]{:S(2)}) collective-permute-start(bf16[128,64,128]{2,1,0:T(8,128)(2,1)S(1)} %copy-done), channel_id=1, source_target_pairs={{0,1},{1,0},{2,3},{3,2},{4,5},{5,4},{6,7},{7,6}} | collective-permute-start | bytes 6291464 | tf_op jit(solution)/shard_map/ppermute | solution.py:378
  670.6 118.6 %collective-permute-start.7 = (bf16[128,64,128]{2,1,0:T(8,128)(2,1)}, bf16[128,64,128]{2,1,0:T(8,128)(2,1)}, u32[]{:S(2)}, u32[]{:S(2)}) collective-permute-start(bf16[128,64,128]{2,1,0:T(8,128)(2,1)} %get-tuple-element.66.refs_6_), channel_id=1, source_target_pairs={{0,2},{1,3},{2,0},{3,1},{4,6},{5,7},{6,4},{7,5}} | collective-permute-start | bytes 6291464 | tf_op jit(solution)/shard_map/ppermute | solution.py:378
  671.0 118.2 %collective-permute-start.8 = (bf16[128,64,128]{2,1,0:T(8,128)(2,1)}, bf16[128,64,128]{2,1,0:T(8,128)(2,1)}, u32[]{:S(2)}, u32[]{:S(2)}) collective-permute-start(bf16[128,64,128]{2,1,0:T(8,128)(2,1)} %get-tuple-element.67.refs_7_), channel_id=1, source_target_pairs={{0,3},{1,2},{2,1},{3,0},{4,7},{5,6},{6,5},{7,4}} | collective-permute-start | bytes 6291464 | tf_op jit(solution)/shard_map/ppermute | solution.py:378
  (4 other events, 34.8 us)
where the time goes:
time: 928 us; the launch traced here: 927 us
  Pallas kernels  655 us (71%)
  waiting for transfers between devices  205 us (22%)
  local copies, waits for them, and re-layouts  30 us (3%)
  blocking collectives  16.5 us (2%)
  starting transfers between devices  11.6 us (1%)
    pallas_call x4, Pallas kernels, middle(): pl.pallas_call(functools.partial(middle_kernel, n_mul, n_mid), grid_spec=...  222 us
    ppermute x15, waiting for transfers between devices, local_step(): lax.ppermute(arr, 'dap', [(d, d ^ bit) for d in range(n_dap)])  205 us
    pallas_call x2, Pallas kernels, final(): pl.pallas_call(functools.partial(final_kernel, bool(seeds)), grid_spec=pl...  171 us
    pallas_call x3, Pallas kernels, project(): pl.pallas_call(functools.partial(project_kernel, keep_norm), grid=(rows /...  164 us
    pallas_call x2, Pallas kernels, grad_b(): pl.pallas_call(functools.partial(grad_b_kernel, len(grads), len(acts)), g...  63 us
    pallas_call x1, Pallas kernels, grad_a(): pl.pallas_call(functools.partial(grad_a_kernel, len(grads), len(acts)), g...  34.9 us
  transfers between devices with their start and end apart: 15, of which 4 were waited for; matrix products, arithmetic and copies ran while one was open for 3% of the time, Pallas kernels for 45%

commit v1 on v0

--- a/solution.py
+++ b/solution.py
@@ -12,11 +12,10 @@
 LANES = 128
 ROWS = 16
 CH_STEP = 8
+MID_CH = 16
+MID_ROWS = 32
+GROUP = 16
 VMEM_LIMIT = 60 * 1024 * 1024
-
-
-def sigmoid(x_val):
-    return 1.0 / (1.0 + jnp.exp(-x_val))
 
 
 def col_mean(x_val):
@@ -43,7 +42,26 @@
     return x_hat, inv_std, (x_hat * scale + offset).astype(BF16)
 
 
-def project_kernel(keep_norm, z_ref, mask_ref, w_ref, bias_ref, scale_ref, offset_ref, *refs):
+def with_bias(mat, vec):
+    pad = jnp.zeros((mat.shape[0], LANES - 1), BF16)
+    return jnp.concatenate([mat, vec[:, None], pad], axis=1)
+
+
+def by_group(arr):
+    split = arr.reshape(arr.shape[:-1] + (4, -1, GROUP))
+    return jnp.swapaxes(split, -3, -2).reshape(arr.shape)
+
+
+def from_group(arr):
+    split = arr.reshape(arr.shape[:-1] + (-1, 4, GROUP))
+    return jnp.swapaxes(split, -3, -2).reshape(arr.shape)
+
+
+def ones_row(width):
+    return (lax.broadcasted_iota(jnp.int32, (LANES, width), 0) == 0).astype(F32).astype(BF16)
+
+
+def project_kernel(keep_norm, z_ref, mask_ref, w_ref, scale_ref, offset_ref, *refs):
     refs = refs[-5:] if keep_norm else refs[-4:]
     a_ref, b_ref = refs[:2]
     scr_a, scr_b = refs[-2:]
@@ -51,6 +69,7 @@
     chans = z_ref.shape[2]
     pitch = ROWS + 1
     plane = chans * pitch
+    one16 = ones_row(256)
 
     def row(i, carry):
         for half in range(n_lane // 2):
@@ -58,15 +77,14 @@
             _, _, znt = input_norm(z_ref[i, cols, :], scale_ref[...], offset_ref[...])
             if keep_norm:
                 refs[2][i, cols, :] = jnp.transpose(znt)
-            proj = dot_nn(w_ref[...], znt) + bias_ref[...]
-            mask_f = jnp.concatenate([mask_ref[i, half * 2 + t] for t in range(2)], axis=1).astype(F32)
-            act_a = mask_f * sigmoid(proj[2 * chans:3 * chans]) * proj[:chans]
-            act_b = mask_f * sigmoid(proj[3 * chans:]) * proj[chans:2 * chans]
-            for t in range(2):
-                base = (half * 2 + t) * plane
-                part = slice(t * LANES, (t + 1) * LANES)
-                scr_a[pl.ds(base + i, chans, stride=pitch), :] = act_a[:, part]
-                scr_b[pl.ds(base + i, chans, stride=pitch), :] = act_b[:, part]
+            mask16 = jnp.concatenate([mask_ref[i, half * 2 + t] for t in range(2)], axis=1).astype(F32).astype(BF16)
+            proj = dot_nn(w_ref[...], jnp.concatenate([znt * mask16, one16 * mask16], axis=0))
+            for g in range(chans // GROUP):
+                pa, pb, la, lb = [proj[(4 * g + n) * GROUP:(4 * g + n + 1) * GROUP] for n in range(4)]
+                for scr, val in ((scr_a, jax.nn.sigmoid(la) * pa), (scr_b, jax.nn.sigmoid(lb) * pb)):
+                    for t in range(2):
+                        at = (half * 2 + t) * plane + g * GROUP * pitch + i
+                        scr[pl.ds(at, GROUP, stride=pitch), :] = val[:, t * LANES:(t + 1) * LANES]
         return carry
 
     lax.fori_loop(0, ROWS, row, 0)
@@ -82,7 +100,7 @@
     lax.fori_loop(0, chans, pack, 0, unroll=4)
 
 
-def project(z_rows, mask_rows, first, rows, w_t, bias, scale, offset, keep_norm, after=()):
+def project(z_rows, mask_rows, first, rows, w_t, scale, offset, keep_norm, after=()):
     _, n_col, chans = z_rows.shape
     z_from, m_from = (0 if z_rows.shape[0] == rows else first // ROWS), first // ROWS
     full = lambda arr: pl.BlockSpec(arr.shape, lambda s: (0,) * arr.ndim)
@@ -101,17 +119,17 @@
         in_specs=[
             pair_spec,
             pl.BlockSpec((ROWS,) + mask_rows.shape[1:], lambda s: (s + m_from, 0, 0, 0)),
-            full(w_t), full(bias), full(scale), full(offset)] + [pl.BlockSpec(memory_space=pl.ANY)] * len(after),
+            full(w_t), full(scale), full(offset)] + [pl.BlockSpec(memory_space=pl.ANY)] * len(after),
         out_specs=out_specs,
         out_shape=out_shape,
         scratch_shapes=[scratch, scratch],
         compiler_params=pltpu.CompilerParams(vmem_limit_bytes=VMEM_LIMIT),
         cost_estimate=pl.CostEstimate(flops=rows * 2 * 10 ** 8, bytes_accessed=rows * 2 ** 19, transcendentals=0),
         name='project',
-    )(z_rows, mask_rows, w_t, bias, scale, offset, *after)
-
-
-def middle_kernel(n_mul, n_mid, idx_ref, a_ref, b0_ref, b1_ref, zn0_ref, zn1_ref, dy0_ref, dy1_ref, wg_ref, bg_ref, wo_ref, wot_ref, bo_ref, scale_ref, offset_ref, *refs):
+    )(z_rows, mask_rows, w_t, scale, offset, *after)
+
+
+def middle_kernel(n_mul, n_mid, idx_ref, a_ref, b0_ref, b1_ref, zn0_ref, zn1_ref, dy0_ref, dy1_ref, wg_ref, wo_ref, wot_ref, scale_ref, offset_ref, *refs):
     do0_ref, do1_ref, gl_ref, dwo_ref, dwg_ref, vec_ref, scr = refs[-7:]
     step = pl.program_id(0)
     tile = LANES
@@ -119,6 +137,9 @@
     pitch = tile + 1
     chans = wo_ref.shape[0]
 
+    one16 = ones_row(2 * tile)
+    one_col = (lax.broadcasted_iota(jnp.int32, (2 * tile, LANES), 1) == 0).astype(F32).astype(BF16)
+
     @pl.when(step == 0)
     def _():
         dwo_ref[...] = jnp.zeros_like(dwo_ref)
@@ -127,13 +148,13 @@
 
     @pl.when(step < n_mul)
     def _():
-        for j in range(CH_STEP):
-            at = (step * CH_STEP + j) * pitch
+        for j in range(MID_CH):
+            at = (step * MID_CH + j) * pitch
             scr[pl.ds(at, tile), :] = dot_nt(a_ref[j], jnp.concatenate([b0_ref[j], b1_ref[j]], axis=0))
 
     @pl.when((step >= n_mul) & (step < n_mul + n_mid))
     def _():
-        first = (step - n_mul) * ROWS
+        first = (step - n_mul) * MID_ROWS
 
         def pair(h, carry):
             r0 = first + 2 * h
@@ -142,9 +163,9 @@
             inv_std = lax.rsqrt(col_mean(centered * centered) + LN_EPS)
             o_hat = centered * inv_std
             o_norm = (o_hat * scale_ref[...] + offset_ref[...]).astype(BF16)
-            update = (dot_nn(wot_ref[...], o_norm) + bo_ref[...]).astype(BF16).astype(F32)
+            update = dot_nn(wot_ref[...], jnp.concatenate([o_norm, one16], axis=0)).astype(BF16).astype(F32)
             zn = jnp.concatenate([ref[2 * h + t] for t in range(2) for ref in (zn0_ref, zn1_ref)], axis=0)
-            sig_g = sigmoid(dot_nt(wg_ref[...], zn) + bg_ref[...])
+            sig_g = jax.nn.sigmoid(dot_nt(wg_ref[...], jnp.concatenate([zn, one_col], axis=1)))
             dy_t = jnp.transpose(jnp.concatenate([ref[2 * h + t].astype(F32) for t in range(2) for ref in (dy0_ref, dy1_ref)], axis=0))
             d_update = (sig_g * dy_t).astype(BF16)
             d_gate = dy_t * update * sig_g * (1.0 - sig_g)
@@ -166,29 +187,29 @@
             dwg_ref[...] += dot_nn(gate16, zn)
             return carry
 
-        lax.fori_loop(0, ROWS // 2, pair, 0)
+        lax.fori_loop(0, MID_ROWS // 2, pair, 0)
 
     @pl.when(step >= n_mul + n_mid)
     def _():
-        for j in range(CH_STEP):
-            at = ((step - n_mul - n_mid) * CH_STEP + j) * pitch
+        for j in range(MID_CH):
+            at = ((step - n_mul - n_mid) * MID_CH + j) * pitch
             do_t = jnp.transpose(scr[pl.ds(at, tile), :]).astype(BF16)
             do0_ref[j] = do_t[:half]
             do1_ref[j] = do_t[half:]
 
 
-def middle(pieces, act_a, b_parts, zn, dy_rows, wg_t, bg, wo, wo_t, bo, scale, offset, after=()):
+def middle(pieces, act_a, b_parts, zn, dy_rows, wg_t, wo, wo_t, scale, offset, after=()):
     chans, rows, n_col = act_a.shape
     half = LANES // 2
-    n_mul = chans // CH_STEP
-    n_mid = rows // ROWS
+    n_mul = chans // MID_CH
+    n_mid = rows // MID_ROWS
     mul_at = lambda s: jnp.minimum(s, n_mul - 1)
     mid_at = lambda s: jnp.clip(s - n_mul, 0, n_mid - 1)
     out_at = lambda s: jnp.maximum(s - n_mul - n_mid, 0)
     full = lambda shape: pl.BlockSpec(shape, lambda s, q: (0,) * len(shape))
-    part_spec = lambda at: pl.BlockSpec((CH_STEP, half, n_col), lambda s, q: (mul_at(s), at, 0))
-    piece_spec = lambda n: pl.BlockSpec((ROWS, half, chans), lambda s, q: (mid_at(s), q[n], 0))
-    do_spec = pl.BlockSpec((CH_STEP, half, rows), lambda s, q: (out_at(s), 0, 0))
+    part_spec = lambda at: pl.BlockSpec((MID_CH, half, n_col), lambda s, q: (mul_at(s), at, 0))
+    piece_spec = lambda n: pl.BlockSpec((MID_ROWS, half, chans), lambda s, q: (mid_at(s), q[n], 0))
+    do_spec = pl.BlockSpec((MID_CH, half, rows), lambda s, q: (out_at(s), 0, 0))
     do_type = jax.ShapeDtypeStruct((chans, half, rows), BF16)
     mats = jax.ShapeDtypeStruct((chans, chans), F32)
     return pl.pallas_call(
@@ -197,14 +218,14 @@
             num_scalar_prefetch=1,
             grid=(2 * n_mul + n_mid,),
             in_specs=[
-                pl.BlockSpec((CH_STEP, rows, n_col), lambda s, q: (mul_at(s), 0, 0)),
+                pl.BlockSpec((MID_CH, rows, n_col), lambda s, q: (mul_at(s), 0, 0)),
                 part_spec(b_parts[0][1]), part_spec(b_parts[1][1]),
                 piece_spec(0), piece_spec(1), piece_spec(0), piece_spec(1),
-                full(wg_t.shape), full(bg.shape), full(wo.shape), full(wo_t.shape), full(bo.shape), full(scale.shape), full(offset.shape)]
+                full(wg_t.shape), full(wo.shape), full(wo_t.shape), full(scale.shape), full(offset.shape)]
             + [pl.BlockSpec(memory_space=pl.ANY)] * len(after),
             out_specs=[
                 do_spec, do_spec,
-                pl.BlockSpec((ROWS, chans, LANES), lambda s, q: (mid_at(s), 0, 0)),
+                pl.BlockSpec((MID_ROWS, chans, LANES), lambda s, q: (mid_at(s), 0, 0)),
                 full((chans, chans)), full((chans, chans)), full((4, chans, LANES))],
             scratch_shapes=[pltpu.VMEM((chans * (LANES + 1), LANES), F32)],
         ),
@@ -215,7 +236,7 @@
         compiler_params=pltpu.CompilerParams(vmem_limit_bytes=VMEM_LIMIT),
         cost_estimate=pl.CostEstimate(flops=25 * 10 ** 9, bytes_accessed=48 * 2 ** 20, transcendentals=0),
         name='middle',
-    )(pieces, act_a, b_parts[0][0], b_parts[1][0], zn, zn, dy_rows, dy_rows, wg_t, bg, wo, wo_t, bo, scale, offset, *after)
+    )(pieces, act_a, b_parts[0][0], b_parts[1][0], zn, zn, dy_rows, dy_rows, wg_t, wo, wo_t, scale, offset, *after)
 
 
 def grad_a_kernel(n_do, n_act, *refs):
@@ -267,7 +288,7 @@
     )(*grads, *acts, mask_f, *after)
 
 
-def final_kernel(seeded, q_ref, z_ref, dy_ref, da_ref, db_ref, gl0, gl1, gl2, gl3, w_ref, wb_ref, bias_ref, scale_ref, offset_ref, *refs):
+def final_kernel(seeded, q_ref, z_ref, dy_ref, da_ref, db_ref, gl0, gl1, gl2, gl3, w_ref, wb_ref, scale_ref, offset_ref, *refs):
     dz_ref, dw_ref, dbin_ref, vec_ref, scr_a, scr_b = refs[-6:]
     gls = (gl0, gl1, gl2, gl3)
     chans = z_ref.shape[2]
@@ -286,6 +307,8 @@
             dbin_ref[...] = jnp.zeros_like(dbin_ref)
             vec_ref[...] = jnp.zeros_like(vec_ref)
 
+    one16 = ones_row(n_lane * LANES)
+
     def unpack(c, carry):
         for t in range(n_lane):
             lanes = slice(t * LANES, (t + 1) * LANES)
@@ -297,54 +320,55 @@
     lax.fori_loop(0, chans, unpack, 0, unroll=4)
 
     def row(i, carry):
-        for half in range(n_lane // 2):
-            qs = [q_ref[2 * half + t] for t in range(2)]
-            offs = [pl.multiple_of(q * LANES, LANES) for q in qs]
-            z_rows = jnp.concatenate([z_ref[i, pl.ds(off, LANES), :] for off in offs], axis=0)
-            x_hat, inv_std, znt = input_norm(z_rows, scale_ref[...], offset_ref[...])
-            proj = dot_nn(w_ref[...], znt) + bias_ref[...]
-            grad_a = jnp.concatenate([scr_a[pl.ds(q * plane + i, chans, stride=pitch), :] for q in qs], axis=1)
-            grad_b = jnp.concatenate([scr_b[pl.ds(q * plane + i, chans, stride=pitch), :] for q in qs], axis=1)
-            sig_a = sigmoid(proj[2 * chans:3 * chans])
-            sig_b = sigmoid(proj[3 * chans:])
-            gs_a = grad_a * sig_a
-            gs_b = grad_b * sig_b
-            d_proj = jnp.concatenate([gs_a, gs_b, gs_a * proj[:chans] * (1.0 - sig_a), gs_b * proj[chans:2 * chans] * (1.0 - sig_b)], axis=0)
-            dbin_ref[...] += d_proj[:, :LANES] + d_proj[:, LANES:]
-            gate = [gls[2 * half + t][i] for t in range(2)]
-            if half:
-                gate = [g[:, part] for part in (slice(0, side), slice(side, LANES)) for g in gate]
-            gate = jnp.concatenate(gate, axis=1)
-            grad16 = d_proj.astype(BF16)
-            dw_ref[...] += dot_nt(grad16, znt)
-            d_znorm = dot_nn(wb_ref[...], jnp.concatenate([grad16, gate], axis=0)).astype(BF16).astype(F32)
-            d_sc = d_znorm * x_hat
-            vec_ref[0] += d_sc[:, :LANES] + d_sc[:, LANES:]
-            vec_ref[1] += d_znorm[:, :LANES] + d_znorm[:, LANES:]
-            grad_hat = d_znorm * scale_ref[...]
-            d_in = inv_std * (grad_hat - col_mean(grad_hat) - x_hat * col_mean(grad_hat * x_hat))
-            d_rows = jnp.transpose(d_in)
-            for t in range(2):
-                out = d_rows[t * LANES:(t + 1) * LANES] + dy_ref[i, pl.ds(offs[t], LANES), :].astype(F32)
-                dz_ref[i, pl.ds(offs[t], LANES), :] = out.astype(BF16)
+        qs = [q_ref[t] for t in range(n_lane)]
+        offs = [pl.multiple_of(q * LANES, LANES) for q in qs]
+        fold = lambda val: sum(val[:, t * LANES:(t + 1) * LANES] for t in range(n_lane))
+        z_rows = jnp.concatenate([z_ref[i, pl.ds(off, LANES), :] for off in offs], axis=0)
+        x_hat, inv_std, znt = input_norm(z_rows, scale_ref[...], offset_ref[...])
+        proj = dot_nn(w_ref[...], jnp.concatenate([znt, one16], axis=0))
+        grad16 = []
+        for g in range(chans // GROUP):
+            parts = [proj[(4 * g + n) * GROUP:(4 * g + n + 1) * GROUP] for n in range(4)]
+            vals = [None] * 4
+            for n, scr in enumerate((scr_a, scr_b)):
+                grad = jnp.concatenate([scr[pl.ds(q * plane + g * GROUP * pitch + i, GROUP, stride=pitch), :] for q in qs], axis=1)
+                sig = jax.nn.sigmoid(parts[2 + n])
+                vals[n] = grad * sig
+                vals[2 + n] = vals[n] * parts[n] * (1.0 - sig)
+            for n in range(4):
+                dbin_ref[(4 * g + n) * GROUP:(4 * g + n + 1) * GROUP] += fold(vals[n])
+                grad16.append(vals[n].astype(BF16))
+        grad16 = jnp.concatenate(grad16, axis=0)
+        gate = [g[i] for g in gls[:2]] + [g[i][:, part] for part in (slice(0, side), slice(side, LANES)) for g in gls[2:]]
+        gate = jnp.concatenate(gate, axis=1)
+        dw_ref[...] += dot_nt(znt, grad16)
+        d_znorm = dot_nn(wb_ref[...], jnp.concatenate([grad16, gate], axis=0)).astype(BF16).astype(F32)
+        vec_ref[0] += fold(d_znorm * x_hat)
+        vec_ref[1] += fold(d_znorm)
+        grad_hat = d_znorm * scale_ref[...]
+        d_in = inv_std * (grad_hat - col_mean(grad_hat) - x_hat * col_mean(grad_hat * x_hat))
+        d_rows = jnp.transpose(d_in)
+        for t in range(n_lane):
+            out = d_rows[t * LANES:(t + 1) * LANES] + dy_ref[i, pl.ds(offs[t], LANES), :].astype(F32)
+            dz_ref[i, pl.ds(offs[t], LANES), :] = out.astype(BF16)
         return carry
 
     lax.fori_loop(0, ROWS, row, 0)
 
 
-def final(q_all, z_rows, dy_rows, d_a, d_b, gates, w_t, w_back, bias, scale, offset, first, d_z=None, seeds=()):
+def final(q_all, z_rows, dy_rows, d_a, d_b, gates, w_t, w_back, scale, offset, first, d_z=None, seeds=()):
     _, n_col, chans = z_rows.shape
     n_step = d_b.shape[1] // ROWS
     at = first // ROWS
     full = lambda shape: pl.BlockSpec(shape, lambda s, q: (0,) * len(shape))
     pair_spec = pl.BlockSpec((ROWS, n_col, chans), lambda s, q: (s + at, 0, 0))
     scratch = pltpu.VMEM((n_col // LANES * chans * (ROWS + 1), LANES), F32)
-    sums = [(4 * chans, chans), (4 * chans, LANES), (2, chans, LANES)]
-    args = [q_all, z_rows, dy_rows, d_a, d_b, *gates, w_t, w_back, bias, scale, offset, *seeds]
+    sums = [(chans, 4 * chans), (4 * chans, LANES), (2, chans, LANES)]
+    args = [q_all, z_rows, dy_rows, d_a, d_b, *gates, w_t, w_back, scale, offset, *seeds]
     in_specs = ([pair_spec, pair_spec, pl.BlockSpec((chans, ROWS, n_col), lambda s, q: (0, s + at, 0)),
                  pl.BlockSpec((chans, ROWS, n_col), lambda s, q: (0, s, 0))]
                 + [pl.BlockSpec((ROWS, chans, LANES), lambda s, q: (s + at, 0, 0))] * 4
-                + [full(w_t.shape), full(w_back.shape), full(bias.shape), full(scale.shape), full(offset.shape)]
+                + [full(w_t.shape), full(w_back.shape), full(scale.shape), full(offset.shape)]
                 + [full(seed.shape) for seed in seeds])
     alias = {}
     if d_z is not None:
@@ -376,8 +400,8 @@
     n_dap = lax.axis_size('dap')
     me = lax.axis_index('dap')
     swap = lambda arr, bit: lax.ppermute(arr, 'dap', [(d, d ^ bit) for d in range(n_dap)])
-    w_t = w_in.T
-    bias = lane_bcast(b_in, 256)
+    w_t = with_bias(by_group(w_in).T, by_group(b_in))
+    row_sc, row_of = (lane_bcast(v, z_loc.shape[1]) for v in (ln_in_scale, ln_in_offset))
     in_sc, in_of = lane_bcast(ln_in_scale, 256), lane_bcast(ln_in_offset, 256)
     out_sc, out_of = lane_bcast(ln_out_scale, 256), lane_bcast(ln_out_offset, 256)
     z_far = swap(z_loc, 2)
@@ -388,12 +412,12 @@
     mask_far = swap(mask_loc, 2)
     z_far = [swap(z_loc[:part], 2)]
     z_far.append(swap(lax.optimization_barrier(z_loc)[part:], 2))
-    weights = (w_t, bias, in_sc, in_of)
+    weights = (w_t, in_sc, in_of)
     a_0, b_0, zn = project(z_loc, mask_loc, 0, rows, *weights, True)
     b_1 = swap(b_0, 1)
     a_1 = swap(a_0, 1)
     blocks = [me ^ r for r in range(n_dap)]
-    tail = (zn, dy_loc, w_gate.T, lane_bcast(b_gate, 256), w_out, w_out.T, lane_bcast(b_out, 256), out_sc, out_of)
+    tail = (zn, dy_loc, with_bias(w_gate.T, b_gate), w_out, with_bias(w_out.T, b_out), out_sc, out_of)
     pieces = lambda *vals: jnp.stack(vals).astype(jnp.int32)
     mids = [middle(pieces(2 * blocks[0], 2 * blocks[0] + 1), a_0, [(b_0, 0), (b_0, 1)], *tail)]
     mids.append(middle(pieces(2 * blocks[1], 2 * blocks[1] + 1), a_0, [(b_1, 0), (b_1, 1)], *tail, after=(mids[0][5],)))
@@ -409,12 +433,12 @@
         far_out.append([swap(mids[2 + h][0], 2), swap(mids[2 + h][1], 3)])
     grads = [m[n] for m in mids for n in range(2)]
     d_a = grad_a(grads, [b_0, b_1, b_2[0], b_3[0], b_2[1], b_3[1]], mask_f)
-    w_back = jnp.concatenate([w_in, w_gate], axis=1)
+    w_back = jnp.concatenate([by_group(w_in), w_gate], axis=1)
     acts = [a_0, a_1, *a_2, *a_3]
     d_z, seeds = None, ()
     for h in range(2):
         d_b = grad_b([mids[0][h], near_out[h], far_out[h][0], far_out[h][1]], acts, mask_f, h, after=(d_a,) if h == 0 else (seeds[2],))
-        d_z, *seeds = final(jnp.stack(blocks).astype(jnp.int32), z_loc, dy_loc, d_a, d_b, [m[2] for m in mids], w_t, w_back, bias, in_sc, in_of,
+        d_z, *seeds = final(jnp.stack(blocks).astype(jnp.int32), z_loc, dy_loc, d_a, d_b, [m[2] for m in mids], w_t, w_back, row_sc, row_of,
                             h * part, d_z, seeds)
     dw_t, dbin, vecs = seeds
     d_wo = sum(m[3] for m in mids)
@@ -423,7 +447,8 @@
     vec_in = jnp.sum(vecs, axis=-1)
     summed = lax.psum((vec_in[0], vec_in[1], dw_t, jnp.sum(dbin, axis=-1), vec_mid[0], vec_mid[1], d_wo, vec_mid[2], d_wg, vec_mid[3]), 'dap')
     summed = list(summed)
-    summed[2] = summed[2].T
+    summed[2] = from_group(summed[2])
+    summed[3] = from_group(summed[3])
     return (d_z,) + tuple(piece.astype(BF16) for piece in summed)
 
 

time: 928 us -> 880 us (0.948)
  Pallas kernels: 655 us -> 588 us
  waiting for transfers between devices: 205 us -> 223 us
    pallas_call x2, Pallas kernels: 171 us -> 144 us  [final(): pl.pallas_call(functools.partial(final_kernel, bool(seeds)), grid_spec=pl...]
    pallas_call x4, Pallas kernels: 222 us -> 198 us  [middle(): pl.pallas_call(functools.partial(middle_kernel, n_mul, n_mid), grid_spec=...]
    ppermute x15, waiting for transfers between devices: 205 us -> 223 us  [local_step(): lax.ppermute(arr, 'dap', [(d, d ^ bit) for d in range(n_dap)])]
    pallas_call x3, Pallas kernels: 164 us -> 147 us  [project(): pl.pallas_call(functools.partial(project_kernel, keep_norm), grid=(rows /...]
  transfers between devices with their start and end apart: 15 -> 15, of which waited for: 4 -> 4; matrix products, arithmetic and copies ran while one was open for 3% -> 3% of each run, Pallas kernels for 45% -> 43%
where the time goes in v1:
time: 880 us; the launch traced here: 879 us
  Pallas kernels  588 us (67%)
  waiting for transfers between devices  223 us (25%)
  local copies, waits for them, and re-layouts  29.6 us (3%)
  blocking collectives  16.5 us (2%)
  starting transfers between devices  11.5 us (1%)
  other arithmetic  9.88 us (1%)
    ppermute x15, waiting for transfers between devices, local_step(): lax.ppermute(arr, 'dap', [(d, d ^ bit) for d in range(n_dap)])  223 us
    pallas_call x4, Pallas kernels, middle(): pl.pallas_call(functools.partial(middle_kernel, n_mul, n_mid), grid_spec=...  198 us
    pallas_call x3, Pallas kernels, project(): pl.pallas_call(functools.partial(project_kernel, keep_norm), grid=(rows /...  147 us
    pallas_call x2, Pallas kernels, final(): pl.pallas_call(functools.partial(final_kernel, bool(seeds)), grid_spec=pl...  144 us
    pallas_call x2, Pallas kernels, grad_b(): pl.pallas_call(functools.partial(grad_b_kernel, len(grads), len(acts)), g...  63 us
    pallas_call x1, Pallas kernels, grad_a(): pl.pallas_call(functools.partial(grad_a_kernel, len(grads), len(acts)), g...  35 us
  transfers between devices with their start and end apart: 15, of which 4 were waited for; matrix products, arithmetic and copies ran while one was open for 3% of the time, Pallas kernels for 43%

profile of v1, /device:TPU:0, one launch (start us, length us, event | category | flops | bytes accessed | tf_op | source)
XLA Modules:
  0.0 879.1 jit_solution(12812700860305292428)
XLA Ops:
  0.6 2.0 reshape.48.mask_ref
  3.6 1.0 copy.49
  6.0 1.4 broadcast_in_dim.19.scale_ref
  7.4 1.4 broadcast_in_dim.20.offset_ref
  8.8 72.2 %project.3 = (bf16[128,128,512]{2,1,0:T(8,128)(2,1)}, bf16[128,128,512]{2,1,0:T(8,128)(2,1)}, bf16[128,512,128]{2,1,0:T(8,128)(2,1)}) custom-call(bf16[128,512,128]{2,1,0:T(8,128)(2,1)} %z_ref.5, s32[128,4,1,128]{3,2,1,0:T(1,128)} %reshape.48.mask_ref, bf16[512,256]{1,0:T(8,128)(2,1)} %maximum_maximum_fusion.w_ref, f32[128,256]{1,0:T(8,128)} %broadcast_in_dim.19.scale_ref, ...), custom_call_target="tpu_custom_call" | custom-call | flops 25600000000 | bytes 67108864 | tf_op jit(solution)/shard_map/project/pallas_call | solution.py:116
  81.1 0.9 collective-permute-start
  82.0 7.6 slice.24
  89.6 2.5 collective-permute-start.1
  96.0 49.4 %middle.4 = (bf16[128,64,128]{2,1,0:T(8,128)(2,1)}, bf16[128,64,128]{2,1,0:T(8,128)(2,1)}, bf16[128,128,128]{2,1,0:T(8,128)(2,1)}, f32[128,128]{1,0:T(8,128)}, f...) custom-call(s32[2]{0:T(128)} %pad_add_fusion.1.idx_ref, bf16[128,128,512]{2,1,0:T(8,128)(2,1)} %get-tuple-element.50.a_ref.refs_4_, ...), custom_call_target="tpu_custom_call" | custom-call | flops 24999999488 | bytes 50331648 | tf_op jit(solution)/shard_map/middle/pallas_call | solution.py:215
  145.5 49.6 %middle.5 = (bf16[128,64,128]{2,1,0:T(8,128)(2,1)}, bf16[128,64,128]{2,1,0:T(8,128)(2,1)}, bf16[128,128,128]{2,1,0:T(8,128)(2,1)}, f32[128,128]{1,0:T(8,128)}, f...) custom-call(s32[2]{0:T(128)} %pad_add_fusion.2.idx_ref, bf16[128,128,512]{2,1,0:T(8,128)(2,1)} %get-tuple-element.50.a_ref.refs_4_, ...), custom_call_target="tpu_custom_call" | custom-call | flops 24999999488 | bytes 50331648 | tf_op jit(solution)/shard_map/middle/pallas_call | solution.py:215
  195.0 83.9 %collective-permute-done.2.mask_ref = s32[128,4,1,128]{3,2,1,0:T(1,128)S(1)} collective-permute-done((s32[128,4,1,128]{3,2,1,0:T(1,128)S(1)}, s32[128,4,1,128]{3,2,1,0:T(1,128)S(1)}, u32[]{:S(2)}, u32[]{:S(2)}) %collective-permute-start.2) | collective-permute-done | bytes 262176 | tf_op jit(solution)/shard_map/ppermute | solution.py:402
  279.7 37.3 %project.4 = (bf16[128,64,512]{2,1,0:T(8,128)(2,1)}, bf16[128,64,512]{2,1,0:T(8,128)(2,1)}) custom-call(bf16[64,512,128]{2,1,0:T(8,128)(2,1)} %collective-permute-done.1.z_ref, s32[128,4,1,128]{3,2,1,0:T(1,128)} %copy-done.22, bf16[512,256]{1,0:T(8,128)(2,1)} %maximum_maximum_fusion.w_ref, f32[128,256]{1,0:T(8,128)} %broadcast_in_dim.19.scale_ref, ...), custom_call_target="tpu_custom_call" | custom-call | flops 12800000000 | bytes 33554432 | tf_op jit(solution)/shard_map/project/pallas_call | solution.py:116
  317.0 7.7 slice.32
  324.8 1.7 collective-permute-start.4
  327.3 3.2 collective-permute-done.3.b1_ref.refs_11_
  330.5 49.8 %middle.6 = (bf16[128,64,128]{2,1,0:T(8,128)(2,1)}, bf16[128,64,128]{2,1,0:T(8,128)(2,1)}, bf16[128,128,128]{2,1,0:T(8,128)(2,1)}, f32[128,128]{1,0:T(8,128)}, f...) custom-call(s32[2]{0:T(128)} %pad_add_fusion.3.idx_ref, bf16[128,128,512]{2,1,0:T(8,128)(2,1)} %get-tuple-element.50.a_ref.refs_4_, ...), custom_call_target="tpu_custom_call" | custom-call | flops 24999999488 | bytes 50331648 | tf_op jit(solution)/shard_map/middle/pallas_call | solution.py:215
  380.3 127.6 %collective-permute-done.4.z_ref = bf16[64,512,128]{2,1,0:T(8,128)(2,1)} collective-permute-done((bf16[64,512,128]{2,1,0:T(8,128)(2,1)}, bf16[64,512,128]{2,1,0:T(8,128)(2,1)}, u32[]{:S(2)}, u32[]{:S(2)}) %collective-permute-start.4) | collective-permute-done | bytes 8388640 | tf_op jit(solution)/shard_map/ppermute | solution.py:402
  507.9 37.5 %project.5 = (bf16[128,64,512]{2,1,0:T(8,128)(2,1)}, bf16[128,64,512]{2,1,0:T(8,128)(2,1)}) custom-call(bf16[64,512,128]{2,1,0:T(8,128)(2,1)} %collective-permute-done.4.z_ref, s32[128,4,1,128]{3,2,1,0:T(1,128)} %copy-done.22, bf16[512,256]{1,0:T(8,128)(2,1)} %maximum_maximum_fusion.w_ref, f32[128,256]{1,0:T(8,128)} %broadcast_in_dim.19.scale_ref, ...), custom_call_target="tpu_custom_call" | custom-call | flops 12800000000 | bytes 33554432 | tf_op jit(solution)/shard_map/project/pallas_call | solution.py:116
  549.2 1.7 collective-permute-start.13
  551.0 8.0 collective-permute-done.5.b1_ref.refs_13_
  559.0 1.5 collective-permute-start.14
  560.5 49.6 %middle.7 = (bf16[128,64,128]{2,1,0:T(8,128)(2,1)}, bf16[128,64,128]{2,1,0:T(8,128)(2,1)}, bf16[128,128,128]{2,1,0:T(8,128)(2,1)}, f32[128,128]{1,0:T(8,128)}, f...) custom-call(s32[2]{0:T(128)} %pad_add_fusion.4.idx_ref, bf16[128,128,512]{2,1,0:T(8,128)(2,1)} %get-tuple-element.50.a_ref.refs_4_, ...), custom_call_target="tpu_custom_call" | custom-call | flops 24999999488 | bytes 50331648 | tf_op jit(solution)/shard_map/middle/pallas_call | solution.py:215
  610.2 1.1 add_reduce_fusion
  612.3 35.0 %grad_a.1.refs_11_.da_ref = bf16[128,128,512]{2,1,0:T(8,128)(2,1)} custom-call(bf16[128,64,128]{2,1,0:T(8,128)(2,1)} %get-tuple-element.53.refs_0_, bf16[128,64,128]{2,1,0:T(8,128)(2,1)} %get-tuple-element.54.refs_1_.refs_0_, bf16[128,64,128]{2,1,0:T(8,128)(2,1)} %get-tuple-element.56.refs_2_, bf16[128,64,128]{2,1,0:T(8,128)(2,1)} %get-tuple-element.57.refs_3_, ...), custom_call_target="tpu_custom_call" | custom-call | flops 15000000512 | bytes 100663296 | tf_op jit(solution)/shard_map/grad_a/pallas_call | solution.py:254
  648.1 1.1 collective-permute-start.8
  649.2 31.5 %grad_b.2.db_ref = bf16[128,64,512]{2,1,0:T(8,128)(2,1)} custom-call(bf16[128,64,128]{2,1,0:T(8,128)(2,1)} %get-tuple-element.53.refs_0_, bf16[128,64,128]{2,1,0:T(8,128)(2,1)} %collective-permute-done.12.refs_1_, bf16[128,64,128]{2,1,0:T(8,128)(2,1)} %collective-permute-done.13.refs_2_, bf16[128,64,128]{2,1,0:T(8,128)(2,1)} %collective-permute-done.14.refs_3_, ...), custom_call_target="tpu_custom_call" | custom-call | flops 8000000000 | bytes 79691776 | tf_op jit(solution)/shard_map/grad_b/pallas_call | solution.py:278
  682.4 71.9 %final.2 = (bf16[128,512,128]{2,1,0:T(8,128)(2,1)}, f32[128,512]{1,0:T(8,128)}, f32[512,128]{1,0:T(8,128)}, f32[2,128,128]{2,1,0:T(8,128)}) custom-call(s32[4]{0:T(128)} %pad_add_fusion.q_ref, bf16[128,512,128]{2,1,0:T(8,128)(2,1)} %z_ref.5, bf16[128,512,128]{2,1,0:T(8,128)(2,1)} %dy_ref.3, bf16[128,128,512]{2,1,0:T(8,128)(2,1)} %grad_a.1.refs_11_.da_ref, ...), custom_call_target="tpu_custom_call" | custom-call | flops 30000001024 | bytes 67108864 | tf_op jit(solution)/shard_map/final/pallas_call | solution.py:378
  754.4 31.5 %grad_b.3.db_ref = bf16[128,64,512]{2,1,0:T(8,128)(2,1)} custom-call(bf16[128,64,128]{2,1,0:T(8,128)(2,1)} %get-tuple-element.54.refs_1_.refs_0_, bf16[128,64,128]{2,1,0:T(8,128)(2,1)} %collective-permute-done.6.refs_1_, bf16[128,64,128]{2,1,0:T(8,128)(2,1)} %collective-permute-done.7.refs_2_, bf16[128,64,128]{2,1,0:T(8,128)(2,1)} %collective-permute-done.8.refs_3_, ...), custom_call_target="tpu_custom_call" | custom-call | flops 8000000000 | bytes 79691776 | tf_op jit(solution)/shard_map/grad_b/pallas_call | solution.py:278
  785.9 72.2 %final.3 = (bf16[128,512,128]{2,1,0:T(8,128)(2,1)}, f32[128,512]{1,0:T(8,128)}, f32[512,128]{1,0:T(8,128)}, f32[2,128,128]{2,1,0:T(8,128)}) custom-call(s32[4]{0:T(128)} %pad_add_fusion.q_ref, bf16[128,512,128]{2,1,0:T(8,128)(2,1)} %z_ref.5, bf16[128,512,128]{2,1,0:T(8,128)(2,1)} %dy_ref.3, ...), custom_call_target="tpu_custom_call", output_to_operand_aliasing={{0}: (16, {})} | custom-call | flops 30000001024 | bytes 67108864 | tf_op jit(solution)/shard_map/final/pallas_call | solution.py:378
  858.1 1.0 reduce_sum.27
  859.1 1.1 reduce_sum.28
  860.2 16.5 %all-reduce.2 = (bf16[128]{0:T(256)(128)(2,1)}, bf16[128]{0:T(256)(128)(2,1)}, bf16[128,512]{1,0:T(8,128)(2,1)S(1)}, bf16[512]{0:T(512)(128)(2,1)S(1)}, bf16[128...) all-reduce(f32[128]{0:T(128)S(1)} %get-tuple-element.137, ...), channel_id=1, replica_groups=mesh['batch'=2,'dap'=4] {'dap'}, use_global_device_ids=true, to_apply=%region_1.0 | all-reduce | flops 99584 | bytes 597504 | tf_op jit(solution)/shard_map/psum | solution.py:448
  (100 shorter events, 17.2 us)
Async XLA Ops:
  81.1 11.5 %copy-start.9 = (bf16[128,128]{1,0:T(8,128)(2,1)S(1)}, bf16[128,128]{1,0:T(8,128)(2,1)}, u32[]{:S(2)}) copy-start(bf16[128,128]{1,0:T(8,128)(2,1)} %param.24) | copy-start | bytes 98308
  81.1 13.5 %copy-start.20 = (bf16[128]{0:T(256)(128)(2,1)S(1)}, bf16[128]{0:T(256)(128)(2,1)}, u32[]{:S(2)}) copy-start(bf16[128]{0:T(256)(128)(2,1)} %param.20) | copy-start | bytes 772
  81.1 14.2 %copy-start.21 = (bf16[128]{0:T(256)(128)(2,1)S(1)}, bf16[128]{0:T(256)(128)(2,1)}, u32[]{:S(2)}) copy-start(bf16[128]{0:T(256)(128)(2,1)} %param.21) | copy-start | bytes 772
  81.1 64.4 %collective-permute-start = (bf16[128,128,512]{2,1,0:T(8,128)(2,1)}, bf16[128,128,512]{2,1,0:T(8,128)(2,1)}, u32[]{:S(2)}, u32[]{:S(2)}) collective-permute-start(bf16[128,128,512]{2,1,0:T(8,128)(2,1)} %get-tuple-element.51.b0_ref.b1_ref.refs_8_), channel_id=1, source_target_pairs={{0,1},{1,0},{2,3},{3,2},{4,5},{5,4},{6,7},{7,6}} | collective-permute-start | bytes 50331656 | tf_op jit(solution)/shard_map/ppermute | solution.py:402
  89.6 189.4 %collective-permute-start.1 = (bf16[64,512,128]{2,1,0:T(8,128)(2,1)}, bf16[64,512,128]{2,1,0:T(8,128)(2,1)}, u32[]{:S(2)}, u32[]{:S(2)}) collective-permute-start(bf16[64,512,128]{2,1,0:T(8,128)(2,1)} %slice.24), channel_id=1, source_target_pairs={{0,2},{1,3},{2,0},{3,1},{4,6},{5,7},{6,4},{7,5}} | collective-permute-start | bytes 25165832 | tf_op jit(solution)/shard_map/ppermute | solution.py:402
  92.1 186.9 %collective-permute-start.2 = (s32[128,4,1,128]{3,2,1,0:T(1,128)S(1)}, s32[128,4,1,128]{3,2,1,0:T(1,128)S(1)}, u32[]{:S(2)}, u32[]{:S(2)}) collective-permute-start(s32[128,4,1,128]{3,2,1,0:T(1,128)S(1)} %copy-done.6), channel_id=1, source_target_pairs={{0,2},{1,3},{2,0},{3,1},{4,6},{5,7},{6,4},{7,5}} | collective-permute-start | bytes 786440 | tf_op jit(solution)/shard_map/ppermute | solution.py:402
  317.0 13.5 %collective-permute-start.3 = (bf16[128,64,512]{2,1,0:T(8,128)(2,1)}, bf16[128,64,512]{2,1,0:T(8,128)(2,1)}, u32[]{:S(2)}, u32[]{:S(2)}) collective-permute-start(bf16[128,64,512]{2,1,0:T(8,128)(2,1)} %get-tuple-element.59.b0_ref.refs_10_), channel_id=1, source_target_pairs={{0,1},{1,0},{2,3},{3,2},{4,5},{5,4},{6,7},{7,6}} | collective-permute-start | bytes 25165832 | tf_op jit(solution)/shard_map/ppermute | solution.py:402
  324.8 183.2 %collective-permute-start.4 = (bf16[64,512,128]{2,1,0:T(8,128)(2,1)}, bf16[64,512,128]{2,1,0:T(8,128)(2,1)}, u32[]{:S(2)}, u32[]{:S(2)}) collective-permute-start(bf16[64,512,128]{2,1,0:T(8,128)(2,1)} %slice.32), channel_id=1, source_target_pairs={{0,2},{1,3},{2,0},{3,1},{4,6},{5,7},{6,4},{7,5}} | collective-permute-start | bytes 25165832 | tf_op jit(solution)/shard_map/ppermute | solution.py:402
  326.5 222.7 %collective-permute-start.9 = (bf16[128,128,512]{2,1,0:T(8,128)(2,1)}, bf16[128,128,512]{2,1,0:T(8,128)(2,1)}, u32[]{:S(2)}, u32[]{:S(2)}) collective-permute-start(bf16[128,128,512]{2,1,0:T(8,128)(2,1)} %get-tuple-element.50.a_ref.refs_4_), channel_id=1, source_target_pairs={{0,1},{1,0},{2,3},{3,2},{4,5},{5,4},{6,7},{7,6}} | collective-permute-start | bytes 50331656 | tf_op jit(solution)/shard_map/ppermute | solution.py:402
  507.9 38.1 %copy-start.4 = (s32[128,512]{1,0:T(8,128)S(1)}, s32[128,512]{1,0:T(8,128)}, u32[]{:S(2)}) copy-start(s32[128,512]{1,0:T(8,128)} %param.14) | copy-start | bytes 786436
  507.9 38.8 %copy-start.2 = (bf16[128,8,4,16]{0,3,2,1:T(8,128)(2,1)S(1)}, bf16[128,8,4,16]{0,3,2,1:T(8,128)(2,1)}, u32[]{:S(2)}) copy-start(bf16[128,8,4,16]{0,3,2,1:T(8,128)(2,1)} %copy-done.1) | copy-start | bytes 393220
  545.5 13.5 %collective-permute-start.5 = (bf16[128,64,512]{2,1,0:T(8,128)(2,1)}, bf16[128,64,512]{2,1,0:T(8,128)(2,1)}, u32[]{:S(2)}, u32[]{:S(2)}) collective-permute-start(bf16[128,64,512]{2,1,0:T(8,128)(2,1)} %get-tuple-element.64.b0_ref.refs_12_), channel_id=1, source_target_pairs={{0,1},{1,0},{2,3},{3,2},{4,5},{5,4},{6,7},{7,6}} | collective-permute-start | bytes 25165832 | tf_op jit(solution)/shard_map/ppermute | solution.py:402
  545.5 102.3 %collective-permute-start.10 = (bf16[128,64,512]{2,1,0:T(8,128)(2,1)}, bf16[128,64,512]{2,1,0:T(8,128)(2,1)}, u32[]{:S(2)}, u32[]{:S(2)}) collective-permute-start(bf16[128,64,512]{2,1,0:T(8,128)(2,1)} %get-tuple-element.60.refs_0_.refs_6_), channel_id=1, source_target_pairs={{0,1},{1,0},{2,3},{3,2},{4,5},{5,4},{6,7},{7,6}} | collective-permute-start | bytes 25165832 | tf_op jit(solution)/shard_map/ppermute | solution.py:402
  546.0 103.2 %collective-permute-start.11 = (bf16[128,64,512]{2,1,0:T(8,128)(2,1)}, bf16[128,64,512]{2,1,0:T(8,128)(2,1)}, u32[]{:S(2)}, u32[]{:S(2)}) collective-permute-start(bf16[128,64,512]{2,1,0:T(8,128)(2,1)} %get-tuple-element.65.refs_0_.refs_7_), channel_id=1, source_target_pairs={{0,1},{1,0},{2,3},{3,2},{4,5},{5,4},{6,7},{7,6}} | collective-permute-start | bytes 25165832 | tf_op jit(solution)/shard_map/ppermute | solution.py:402
  548.7 98.6 %collective-permute-start.12 = (bf16[128,64,128]{2,1,0:T(8,128)(2,1)}, bf16[128,64,128]{2,1,0:T(8,128)(2,1)}, u32[]{:S(2)}, u32[]{:S(2)}) collective-permute-start(bf16[128,64,128]{2,1,0:T(8,128)(2,1)} %get-tuple-element.56.refs_2_), channel_id=1, source_target_pairs={{0,1},{1,0},{2,3},{3,2},{4,5},{5,4},{6,7},{7,6}} | collective-permute-start | bytes 6291464 | tf_op jit(solution)/shard_map/ppermute | solution.py:402
  549.2 98.9 %collective-permute-start.13 = (bf16[128,64,128]{2,1,0:T(8,128)(2,1)}, bf16[128,64,128]{2,1,0:T(8,128)(2,1)}, u32[]{:S(2)}, u32[]{:S(2)}) collective-permute-start(bf16[128,64,128]{2,1,0:T(8,128)(2,1)} %get-tuple-element.61.refs_4_), channel_id=1, source_target_pairs={{0,2},{1,3},{2,0},{3,1},{4,6},{5,7},{6,4},{7,5}} | collective-permute-start | bytes 6291464 | tf_op jit(solution)/shard_map/ppermute | solution.py:402
  559.0 51.2 %copy-start.3 = (f32[4,128,128]{2,1,0:T(8,128)S(1)}, f32[4,128,128]{2,1,0:T(8,128)}, u32[]{:S(2)}) copy-start(f32[4,128,128]{2,1,0:T(8,128)} %get-tuple-element.55.refs_0_) | copy-start | bytes 786436
  559.0 51.2 %copy-start.7 = (f32[4,128,128]{2,1,0:T(8,128)S(1)}, f32[4,128,128]{2,1,0:T(8,128)}, u32[]{:S(2)}) copy-start(f32[4,128,128]{2,1,0:T(8,128)} %get-tuple-element.58.refs_0_) | copy-start | bytes 786436
  559.0 51.2 %copy-start.8 = (f32[4,128,128]{2,1,0:T(8,128)S(1)}, f32[4,128,128]{2,1,0:T(8,128)}, u32[]{:S(2)}) copy-start(f32[4,128,128]{2,1,0:T(8,128)} %get-tuple-element.63.refs_0_) | copy-start | bytes 786436
  559.0 52.4 %copy-start.10 = (f32[128,128]{1,0:T(8,128)S(1)}, f32[128,128]{1,0:T(8,128)}, u32[]{:S(2)}) copy-start(f32[128,128]{1,0:T(8,128)} %get-tuple-element.81) | copy-start | bytes 196612
  559.0 52.4 %copy-start.11 = (f32[128,128]{1,0:T(8,128)S(1)}, f32[128,128]{1,0:T(8,128)}, u32[]{:S(2)}) copy-start(f32[128,128]{1,0:T(8,128)} %get-tuple-element.85) | copy-start | bytes 196612
  559.0 52.4 %copy-start.12 = (f32[128,128]{1,0:T(8,128)S(1)}, f32[128,128]{1,0:T(8,128)}, u32[]{:S(2)}) copy-start(f32[128,128]{1,0:T(8,128)} %get-tuple-element.82) | copy-start | bytes 196612
  559.0 52.4 %copy-start.13 = (f32[128,128]{1,0:T(8,128)S(1)}, f32[128,128]{1,0:T(8,128)}, u32[]{:S(2)}) copy-start(f32[128,128]{1,0:T(8,128)} %get-tuple-element.86) | copy-start | bytes 196612
  559.0 52.4 %copy-start.14 = (f32[128,128]{1,0:T(8,128)S(1)}, f32[128,128]{1,0:T(8,128)}, u32[]{:S(2)}) copy-start(f32[128,128]{1,0:T(8,128)} %get-tuple-element.83) | copy-start | bytes 196612
  559.0 52.4 %copy-start.15 = (f32[128,128]{1,0:T(8,128)S(1)}, f32[128,128]{1,0:T(8,128)}, u32[]{:S(2)}) copy-start(f32[128,128]{1,0:T(8,128)} %get-tuple-element.87) | copy-start | bytes 196612
  559.0 90.2 %collective-permute-start.14 = (bf16[128,64,128]{2,1,0:T(8,128)(2,1)}, bf16[128,64,128]{2,1,0:T(8,128)(2,1)}, u32[]{:S(2)}, u32[]{:S(2)}) collective-permute-start(bf16[128,64,128]{2,1,0:T(8,128)(2,1)} %get-tuple-element.62.refs_5_), channel_id=1, source_target_pairs={{0,3},{1,2},{2,1},{3,0},{4,7},{5,6},{6,5},{7,4}} | collective-permute-start | bytes 6291464 | tf_op jit(solution)/shard_map/ppermute | solution.py:402
  612.3 35.0 %copy-start = (bf16[128,64,128]{2,1,0:T(8,128)(2,1)S(1)}, bf16[128,64,128]{2,1,0:T(8,128)(2,1)}, u32[]{:S(2)}) copy-start(bf16[128,64,128]{2,1,0:T(8,128)(2,1)} %get-tuple-element.57.refs_3_) | copy-start | bytes 6291460
  647.3 33.5 %copy-start.16 = (bf16[128]{0:T(256)(128)(2,1)S(1)}, bf16[128]{0:T(256)(128)(2,1)}, u32[]{:S(2)}) copy-start(bf16[128]{0:T(256)(128)(2,1)} %param.16) | copy-start | bytes 772
  647.3 34.3 %copy-start.17 = (bf16[128]{0:T(256)(128)(2,1)S(1)}, bf16[128]{0:T(256)(128)(2,1)}, u32[]{:S(2)}) copy-start(bf16[128]{0:T(256)(128)(2,1)} %param.17) | copy-start | bytes 772
  647.3 107.0 %collective-permute-start.6 = (bf16[128,64,128]{2,1,0:T(8,128)(2,1)S(1)}, bf16[128,64,128]{2,1,0:T(8,128)(2,1)}, u32[]{:S(2)}, u32[]{:S(2)}) collective-permute-start(bf16[128,64,128]{2,1,0:T(8,128)(2,1)S(1)} %copy-done), channel_id=1, source_target_pairs={{0,1},{1,0},{2,3},{3,2},{4,5},{5,4},{6,7},{7,6}} | collective-permute-start | bytes 6291464 | tf_op jit(solution)/shard_map/ppermute | solution.py:402
  647.7 106.6 %collective-permute-start.7 = (bf16[128,64,128]{2,1,0:T(8,128)(2,1)}, bf16[128,64,128]{2,1,0:T(8,128)(2,1)}, u32[]{:S(2)}, u32[]{:S(2)}) collective-permute-start(bf16[128,64,128]{2,1,0:T(8,128)(2,1)} %get-tuple-element.66.refs_6_), channel_id=1, source_target_pairs={{0,2},{1,3},{2,0},{3,1},{4,6},{5,7},{6,4},{7,5}} | collective-permute-start | bytes 6291464 | tf_op jit(solution)/shard_map/ppermute | solution.py:402
  648.1 106.2 %collective-permute-start.8 = (bf16[128,64,128]{2,1,0:T(8,128)(2,1)}, bf16[128,64,128]{2,1,0:T(8,128)(2,1)}, u32[]{:S(2)}, u32[]{:S(2)}) collective-permute-start(bf16[128,64,128]{2,1,0:T(8,128)(2,1)} %get-tuple-element.67.refs_7_), channel_id=1, source_target_pairs={{0,3},{1,2},{2,1},{3,0},{4,7},{5,6},{6,5},{7,4}} | collective-permute-start | bytes 6291464 | tf_op jit(solution)/shard_map/ppermute | solution.py:402
  (6 other events, 46.2 us)
